TPU v7x, 32 devices: a whole 2x2x4 slice. The times are simulated.
32 devices in a mesh: dp: 4 (over z), row: 2 (over y), fsdp: 4 (over x, core).
Axes of the slice: x: 2, y: 2, z: 4, core: 2. Of those that a mesh axis runs over, the one named last changes fastest.
Arguments:
- x_in: bfloat16 [65536, 768], P(('dp', 'row', 'fsdp'))
- dy_out: bfloat16 [65536, 768], P(('dp', 'row', 'fsdp'))
- w_gate: bfloat16 [768, 2048], P(None, ('row', 'fsdp'))
- w_up: bfloat16 [768, 2048], P(None, ('row', 'fsdp'))
- w_down: bfloat16 [2048, 768], P(('row', 'fsdp'))
- g_next: float32 [32, 3, 768, 2048], P(('dp', 'row', 'fsdp'))
Outputs:
- output 1: bfloat16 [65536, 768], P(('dp', 'row', 'fsdp'))
- output 2: float32 [3, 768, 2048], P(None, None, ('row', 'fsdp'))
- output 3: float32 [32, 3, 768, 2048], P(('dp', 'row', 'fsdp'))
All inputs are finite; a program needn't handle non-finite values.
Results may differ from a plain program's by a relative error of at most 0.0139156.
Values are sent between devices in bfloat16 or wider.
A program may use at most 1 GiB of HBM per device.

v0:
```python
import jax
import jax.numpy as jnp
from jax import lax
from jax.sharding import PartitionSpec as P

GROUP_AXES = ("row", "fsdp")
ALL_AXES = ("dp", "row", "fsdp")
CONTRACT_LAST = (((1,), (1,)), ((), ()))
CONTRACT_FIRST = (((0,), (0,)), ((), ()))


def local_backward(x_blk, dy_blk, w_gate, w_up, w_down):
    a_pre = jnp.dot(x_blk, w_gate, preferred_element_type=jnp.float32)
    b_pre = jnp.dot(x_blk, w_up, preferred_element_type=jnp.float32)
    sig_a = jax.nn.sigmoid(a_pre)
    silu_a = a_pre * sig_a
    h_act = (silu_a * b_pre).astype(jnp.bfloat16)
    dh_full = lax.dot_general(dy_blk, w_down, CONTRACT_LAST, preferred_element_type=jnp.float32)
    da_bf = (dh_full * b_pre * sig_a * (1.0 + a_pre * (1.0 - sig_a))).astype(jnp.bfloat16)
    db_bf = (dh_full * silu_a).astype(jnp.bfloat16)
    dx_acc = lax.dot_general(da_bf, w_gate, CONTRACT_LAST, preferred_element_type=jnp.float32) + lax.dot_general(db_bf, w_up, CONTRACT_LAST, preferred_element_type=jnp.float32)
    grad_gate = lax.dot_general(x_blk, da_bf, CONTRACT_FIRST, preferred_element_type=jnp.float32)
    grad_up = lax.dot_general(x_blk, db_bf, CONTRACT_FIRST, preferred_element_type=jnp.float32)
    grad_down = lax.dot_general(dy_blk, h_act, CONTRACT_FIRST, preferred_element_type=jnp.float32)
    return dx_acc.astype(jnp.bfloat16), jnp.stack([grad_gate, grad_up, grad_down])


def solution(mesh):
    def per_device(x_blk, dy_blk, gate_shard, up_shard, down_shard, g_part):
        w_gate = lax.all_gather(gate_shard, GROUP_AXES, axis=1, tiled=True)
        w_up = lax.all_gather(up_shard, GROUP_AXES, axis=1, tiled=True)
        w_down = lax.all_gather(down_shard, GROUP_AXES, axis=0, tiled=True)
        dx_blk, dw_local = local_backward(x_blk, dy_blk, w_gate, w_up, w_down)
        g_summed = lax.psum(g_part[0].astype(jnp.bfloat16), "dp")
        g_shard = lax.psum_scatter(g_summed, GROUP_AXES, scatter_dimension=2, tiled=True)
        return dx_blk, g_shard.astype(jnp.float32), dw_local[None]

    return jax.shard_map(
        per_device,
        mesh=mesh,
        in_specs=(P(ALL_AXES, None), P(ALL_AXES, None), P(None, GROUP_AXES), P(None, GROUP_AXES), P(GROUP_AXES, None), P(ALL_AXES, None, None, None)),
        out_specs=(P(ALL_AXES, None), P(None, None, GROUP_AXES), P(ALL_AXES, None, None, None)),
        check_vma=False,
    )
```

profile of v0, /device:TPU:0, one launch (start us, length us, event | category | flops | bytes accessed | tf_op | source)
XLA Modules:
  0.0 260.2 jit_solution(7835241932273539127)
XLA Ops:
  7.2 0.0 copy-start
  7.2 0.0 all-gather.8.cloned.1.call-start
  7.2 0.7 all-gather.8.cloned.1.call-update
  7.9 0.0 all-gather.6.cloned.1.call-start
  8.0 0.7 all-gather.6.cloned.1.call-update
  8.7 0.0 all-gather.4.cloned.1.call-start
  8.7 0.7 all-gather.4.cloned.1.call-update
  9.4 0.0 reduce-scatter.2.cloned.1.call-start
  9.4 10.1 %convert_bitcast_fusion = bf16[3,768,2048]{2,1,0:T(8,128)(2,1)} fusion(f32[1,3,768,2048]{3,2,1,0:T(8,128)} %param.11), kind=kLoop, calls=%fused_computation.6 | loop fusion | flops 4718592 | bytes 28311552 | tf_op jit(solution)/shard_map/convert_element_type | solution.py:34
  19.5 0.0 reduce-scatter.2.cloned.1.call-update
  19.5 0.0 all-reduce.2.cloned.1.call-start
  19.6 25.5 %all-gather.8.cloned.1.call-done = bf16[768,2048]{1,0:T(8,128)(2,1)} async-done(((bf16[768,256]{1,0:T(8,128)(2,1)}), bf16[768,2048]{1,0:T(8,128)(2,1)}) %all-gather.8.cloned.1.call-update) | async-done | bytes 3145744 | tf_op jit(solution)/shard_map/all_gather | solution.py:30
  45.1 0.0 copy-done
  45.1 11.5 %fusion.6 = f32[2048,2048]{1,0:T(8,128)} fusion(bf16[2048,768]{1,0:T(8,128)(2,1)S(1)} %copy-done, bf16[768,2048]{1,0:T(8,128)(2,1)} %all-gather.8.cloned.1.call-done), kind=kOutput, calls=%fused_computation.14 | convolution fusion | flops 6442450944 | bytes 23068672 | tf_op jit(solution)/shard_map/dot_general | solution.py:13
  56.6 22.8 %all-gather.6.cloned.1.call-done = bf16[768,2048]{1,0:T(8,128)(2,1)} async-done(((bf16[768,256]{1,0:T(8,128)(2,1)}), bf16[768,2048]{1,0:T(8,128)(2,1)}) %all-gather.6.cloned.1.call-update) | async-done | bytes 3145744 | tf_op jit(solution)/shard_map/all_gather | solution.py:31
  79.5 11.4 %fusion.5 = f32[2048,2048]{1,0:T(8,128)} fusion(bf16[2048,768]{1,0:T(8,128)(2,1)S(1)} %copy-done, bf16[768,2048]{1,0:T(8,128)(2,1)} %all-gather.6.cloned.1.call-done), kind=kOutput, calls=%fused_computation.13 | convolution fusion | flops 6442450944 | bytes 23068672 | tf_op jit(solution)/shard_map/dot_general | solution.py:14
  90.9 22.4 %all-gather.4.cloned.1.call-done = bf16[2048,768]{1,0:T(8,128)(2,1)} async-done(((bf16[256,768]{1,0:T(8,128)(2,1)}), bf16[2048,768]{1,0:T(8,128)(2,1)}) %all-gather.4.cloned.1.call-update) | async-done | bytes 3145744 | tf_op jit(solution)/shard_map/all_gather | solution.py:32
  113.3 24.1 %multiply_convert_fusion.1 = (bf16[2048,2048]{1,0:T(8,128)(2,1)}, bf16[2048,2048]{1,0:T(8,128)(2,1)}) fusion(f32[2048,2048]{1,0:T(8,128)} %fusion.6, f32[2048,2048]{1,0:T(8,128)} %fusion.5, bf16[2048,768]{1,0:T(8,128)(2,1)} %param.7, bf16[2048,768]{1,0:T(8,128)(2,1)} %all-gather.4.cloned.1.call-done), kind=kOutput, calls=%fused_computation.2 | convolution fusion | flops 6496976896 | bytes 56623104 | tf_op jit(solution)/shard_map/dot_general | solution.py:18
  137.4 0.0 copy-start.3
  137.4 0.0 copy-start.5
  137.4 11.0 %convolution_bitcast_fusion = f32[1,768,2048]{1,2,0:T(8,128)} fusion(bf16[2048,2048]{1,0:T(8,128)(2,1)} %get-tuple-element.6, bf16[2048,768]{1,0:T(8,128)(2,1)S(1)} %copy-done), kind=kOutput, calls=%fused_computation.10 | convolution fusion | flops 6442450944 | bytes 17825792 | tf_op jit(solution)/shard_map/dot_general | solution.py:23
  148.4 0.0 copy-done.3
  148.4 0.0 copy-done.5
  148.4 0.0 copy-start.4
  148.4 8.8 %fusion.7 = f32[2048,768]{1,0:T(8,128)} fusion(bf16[2048,2048]{1,0:T(8,128)(2,1)S(1)} %copy-done.5, bf16[768,2048]{1,0:T(8,128)(2,1)S(1)} %copy-done.3), kind=kOutput, calls=%fused_computation.15 | convolution fusion | flops 6442450944 | bytes 17825792 | tf_op jit(solution)/shard_map/dot_general | solution.py:21
  157.2 0.0 copy-done.4
  157.2 0.0 copy-start.2
  157.2 12.4 %add_convert_fusion = bf16[2048,768]{1,0:T(8,128)(2,1)} fusion(f32[2048,768]{1,0:T(8,128)} %fusion.7, bf16[2048,2048]{1,0:T(8,128)(2,1)} %get-tuple-element.6, bf16[768,2048]{1,0:T(8,128)(2,1)S(1)} %copy-done.4), kind=kOutput, calls=%fused_computation.8 | convolution fusion | flops 6445596672 | bytes 20971520 | tf_op jit(solution)/shard_map/dot_general | solution.py:21
  169.6 0.0 copy-done.2
  169.6 16.4 %fusion.2 = f32[1,768,2048]{1,2,0:T(8,128)} fusion(bf16[2048,768]{1,0:T(8,128)(2,1)S(1)} %copy-done.2, f32[2048,2048]{1,0:T(8,128)} %fusion.5, f32[2048,2048]{1,0:T(8,128)} %fusion.6), kind=kOutput, calls=%fused_computation.9 | convolution fusion | flops 6467616768 | bytes 42991616 | tf_op jit(solution)/shard_map/dot_general | solution.py:24
  186.0 6.4 %reduce-scatter.2.cloned.1.call-done = bf16[3,768,256]{2,1,0:T(8,128)(2,1)} async-done(((bf16[3,768,2048]{2,1,0:T(8,128)(2,1)}), bf16[3,768,256]{2,1,0:T(8,128)(2,1)}) %reduce-scatter.2.cloned.1.call-update) | async-done | bytes 1179664 | tf_op jit(solution)/shard_map/reduce_scatter | solution.py:35
  192.4 0.0 all-reduce.2.cloned.1.call-update
  192.5 0.0 copy-start.1
  192.5 9.8 %convolution_bitcast_fusion.1 = f32[1,768,2048]{1,2,0:T(8,128)S(1)} fusion(bf16[2048,2048]{1,0:T(8,128)(2,1)} %get-tuple-element.7, bf16[2048,768]{1,0:T(8,128)(2,1)S(1)} %copy-done), kind=kOutput, calls=%fused_computation.11 | convolution fusion | flops 6442450944 | bytes 17825792 | tf_op jit(solution)/shard_map/dot_general | solution.py:22
  202.3 0.0 copy-done.1
  202.3 9.4 %maximum_bitcast_fusion = f32[1,3,768,2048]{2,3,1,0:T(8,128)} fusion(f32[1,768,2048]{1,2,0:T(8,128)S(1)} %copy-done.1, f32[1,768,2048]{1,2,0:T(8,128)} %convolution_bitcast_fusion, f32[1,768,2048]{1,2,0:T(8,128)S(1)} %convolution_bitcast_fusion.1), kind=kLoop, calls=%fused_computation | loop fusion | flops 9437184 | bytes 37748736 | tf_op jit(solution)/shard_map/broadcast_in_dim | solution.py:36
  211.8 18.7 %copy.9 = f32[1,3,768,2048]{3,2,1,0:T(8,128)} copy(f32[1,3,768,2048]{2,3,1,0:T(8,128)} %maximum_bitcast_fusion) | data formatting | bytes 37748736
  230.4 20.4 %all-reduce.2.cloned.1.call-done = bf16[3,768,256]{2,1,0:T(8,128)(2,1)} async-done(((bf16[3,768,256]{2,1,0:T(8,128)(2,1)}), bf16[3,768,256]{2,1,0:T(8,128)(2,1)}) %all-reduce.2.cloned.1.call-update) | async-done | bytes 1179664 | tf_op jit(solution)/shard_map/psum | solution.py:34
  250.8 2.9 %convert_element_type.26 = f32[3,768,256]{2,1,0:T(8,128)} convert(bf16[3,768,256]{2,1,0:T(8,128)(2,1)} %all-reduce.2.cloned.1.call-done) | non-fusion elementwise | flops 589824 | bytes 3538944 | tf_op jit(solution)/shard_map/convert_element_type | solution.py:36
Async XLA Ops:
  7.2 37.9 %copy-start = (bf16[2048,768]{1,0:T(8,128)(2,1)S(1)}, bf16[2048,768]{1,0:T(8,128)(2,1)}, u32[]{:S(2)}) copy-start(bf16[2048,768]{1,0:T(8,128)(2,1)} %param.6) | copy-start | bytes 9437188
  7.2 37.9 %all-gather.8.cloned.1.call-start = ((), (), s32[]{:S(2)}) async-start(), calls=%async_computation.3 | async-start | bytes 3538944 | tf_op jit(solution)/shard_map/all_gather | solution.py:30
  7.9 71.5 %all-gather.6.cloned.1.call-start = ((), (), s32[]{:S(2)}) async-start(), calls=%async_computation.2 | async-start | bytes 3538944 | tf_op jit(solution)/shard_map/all_gather | solution.py:31
  8.7 104.6 %all-gather.4.cloned.1.call-start = ((), (), s32[]{:S(2)}) async-start(), calls=%async_computation.1 | async-start | bytes 3538944 | tf_op jit(solution)/shard_map/all_gather | solution.py:32
  9.4 183.0 %reduce-scatter.2.cloned.1.call-start = ((), (), s32[]{:S(2)}) async-start(), calls=%async_computation.4 | async-start | bytes 10616832 | tf_op jit(solution)/shard_map/reduce_scatter | solution.py:35
  19.5 231.3 %all-reduce.2.cloned.1.call-start = ((), (), s32[]{:S(2)}) async-start(), calls=%async_computation.5 | async-start | bytes 2359296 | tf_op jit(solution)/shard_map/psum | solution.py:34
  137.4 11.0 %copy-start.3 = (bf16[768,2048]{1,0:T(8,128)(2,1)S(1)}, bf16[768,2048]{1,0:T(8,128)(2,1)}, u32[]{:S(2)}) copy-start(bf16[768,2048]{1,0:T(8,128)(2,1)} %all-gather.8.cloned.1.call-done) | copy-start | bytes 9437188
  137.4 11.0 %copy-start.5 = (bf16[2048,2048]{1,0:T(8,128)(2,1)S(1)}, bf16[2048,2048]{1,0:T(8,128)(2,1)}, u32[]{:S(2)}) copy-start(bf16[2048,2048]{1,0:T(8,128)(2,1)} %get-tuple-element.7) | copy-start | bytes 25165828
  148.4 8.8 %copy-start.4 = (bf16[768,2048]{1,0:T(8,128)(2,1)S(1)}, bf16[768,2048]{1,0:T(8,128)(2,1)}, u32[]{:S(2)}) copy-start(bf16[768,2048]{1,0:T(8,128)(2,1)} %all-gather.6.cloned.1.call-done) | copy-start | bytes 9437188
  157.2 12.4 %copy-start.2 = (bf16[2048,768]{1,0:T(8,128)(2,1)S(1)}, bf16[2048,768]{1,0:T(8,128)(2,1)}, u32[]{:S(2)}) copy-start(bf16[2048,768]{1,0:T(8,128)(2,1)} %param.7) | copy-start | bytes 9437188
  192.5 9.9 %copy-start.1 = (f32[1,768,2048]{1,2,0:T(8,128)S(1)}, f32[1,768,2048]{1,2,0:T(8,128)}, u32[]{:S(2)}) copy-start(f32[1,768,2048]{1,2,0:T(8,128)} %fusion.2) | copy-start | bytes 18874372
Sparse Core Ops, SparseCore 0:
  9.9 35.1 all-gather.7
  47.0 32.4 all-gather.5
  81.3 31.8 all-gather.3
  116.6 75.7 reduce-scatter.1
  194.7 56.0 all-reduce.1
where the time goes:
time: 261 us; the launch traced here: 260 us
  matrix products  105 us (40%)
  waiting for transfers between devices  99.7 us (38%)
  other arithmetic  22.4 us (9%)
  local copies, waits for them, and re-layouts  18.7 us (7%)
  between operations  13.8 us (5%)
    all_gather x1, waiting for transfers between devices, per_device(): w_gate = lax.all_gather(gate_shard, GROUP_AXES, axis=1, tiled=True)  25.5 us
    dot_general x1, matrix products, local_backward(): lax.dot_general(dy_blk, w_down, CONTRACT_LAST, preferred_element_type=jnp...  24.1 us
    all_gather x1, waiting for transfers between devices, per_device(): w_up = lax.all_gather(up_shard, GROUP_AXES, axis=1, tiled=True)  22.8 us
    all_gather x1, waiting for transfers between devices, per_device(): w_down = lax.all_gather(down_shard, GROUP_AXES, axis=0, tiled=True)  22.4 us
    psum x1, waiting for transfers between devices, per_device(): g_summed = lax.psum(g_part[0].astype(jnp.bfloat16), 'dp')  20.4 us
    unnamed x13, local copies, waits for them, and re-layouts  18.7 us
    dot_general x1, matrix products, local_backward(): lax.dot_general(dy_blk, h_act, CONTRACT_FIRST, preferred_element_type=jnp...  16.4 us
    dot_general x1, matrix products, local_backward(): lax.dot_general(db_bf, w_up, CONTRACT_LAST, preferred_element_type=jnp.fl...  12.4 us
  transfers between devices with their start and end apart: 5, of which 5 were waited for; matrix products, arithmetic and copies ran while one was open for 55% of the time, Pallas kernels for 0%

commit v1 on v0

v1 whole, which is shorter than its diff:
```python
import functools

import jax
import jax.numpy as jnp
from jax import lax
from jax.experimental import pallas as pl
from jax.experimental.pallas import tpu as pltpu
from jax.sharding import PartitionSpec as P

ALL_AXES = ("dp", "row", "fsdp")
GROUP_AXES = ("row", "fsdp")
LAST = (((1,), (1,)), ((), ()))
F32, BF16 = jnp.float32, jnp.bfloat16

BLOCKS = 8
TILES = 4
UNITS = BLOCKS * TILES
CHUNKS = 18
FIRST = 4
LAGS = (0, 1, 3, 5, 7, 9, 11, 13)
FWD_XY, FWD_D = 6, 12
PASS = (13, 19, 25)
SLOTS = 4


def whole_step(x_hbm, dy_hbm, wg_hbm, wu_hbm, wd_hbm, g_hbm, dx_out, dn_out, dw_out,
               xv, dyv, xt, dyt, w1, w3, w2, dxacc, dwacc,
               gbuf, send_c, own, recv_c, recv_1, recv_2, recv_z1, recv_z2, res,
               ld_sem, g_sem, ws_sem, wr_sem, s_sem, r_sem, dw_sem, out_sem):
    z, y, f = lax.axis_index("dp"), lax.axis_index("row"), lax.axis_index("fsdp")
    x, c = f // 2, f % 2
    z0, z1 = z % 2, z // 2
    act = (z0 + c + 1) % 2
    tile = xv.shape[0] // TILES
    wide = w1.shape[2]
    half_w2 = w2.shape[1] // 2
    rows = gbuf.shape[1]
    rh, rq = rows // 2, rows // 4

    def dev(dz=None, yy=None, xx=None, cc=None):
        zz = z if dz is None else dz
        return (zz, y if yy is None else yy, (x if xx is None else xx) * 2 + (c if cc is None else cc))

    partner = dev(cc=1 - c)
    x_nbr, y_nbr = dev(xx=1 - x), dev(yy=1 - y)
    z_near = dev(dz=z + 1 - 2 * z0)
    z_far = dev(dz=(z + 2) % 4)

    own_loads = [pltpu.make_async_copy(s, d.at[0], ld_sem.at[i]) for i, (s, d) in enumerate(((wg_hbm, w1), (wu_hbm, w3), (wd_hbm, w2)))]
    act_loads = [pltpu.make_async_copy(s, d, ld_sem.at[3 + i]) for i, (s, d) in enumerate(((x_hbm, xv), (dy_hbm, dyv)))]
    for cp in own_loads + act_loads:
        cp.start()

    def g_load(k):
        return pltpu.make_async_copy(g_hbm.at[k], gbuf.at[k % 3], g_sem.at[k % 3])

    g_load(0).start()
    g_load(1).start()

    barrier = pltpu.get_barrier_semaphore()
    for d in (partner, x_nbr, y_nbr, z_near, z_far):
        pl.semaphore_signal(barrier, inc=1, device_id=d, device_id_type=pl.DeviceIdType.MESH)
    pl.semaphore_wait(barrier, 5)

    def part(slot, p):
        if p == 0:
            return w1.at[slot]
        if p == 1:
            return w3.at[slot]
        return w2.at[slot, pl.ds((p - 2) * half_w2, half_w2)]

    def wcopy(src, dst, p, sem, device):
        return pltpu.make_async_remote_copy(
            src_ref=part(src, p), dst_ref=part(dst, p), send_sem=ws_sem.at[sem, p], recv_sem=wr_sem.at[dst, p],
            device_id=device, device_id_type=pl.DeviceIdType.MESH)

    def wwait(slot, p):
        wcopy(slot, slot, p, 0, partner).wait_recv()

    def own_copies():
        return [wcopy(0, 1, p, 0, partner) for p in range(4)]

    def own_far():
        return [wcopy(0, s, p, i, d) for p in range(4) for s, i, d in ((2, 1, x_nbr), (3, 2, y_nbr))]

    def fwd_xy(p):
        near = [wcopy(2, 2, p, 3, z_near), wcopy(3, 3, p, 4, z_near), wcopy(2, 5, p, 5, partner), wcopy(3, 6, p, 6, partner)]
        if p % 2 == 0:
            return [wcopy(2, 4, p, 7, y_nbr)] + near
        return [wcopy(3, 4, p, 7, x_nbr)] + near

    def fwd_d(p):
        return [wcopy(4, 4, p, 8, z_near), wcopy(4, 7, p, 9, partner)]

    for cp in own_loads:
        cp.wait()
    for cp in own_copies():
        cp.start()

    @pl.when(act == 1)
    def _():
        for cp in own_far():
            cp.start()

    for cp in act_loads:
        cp.wait()

    def neighbour(k, stage):
        typ = (k + stage) % 2
        return dev(yy=(y + typ) % 2, xx=(x + 1 - typ) % 2)

    def rcopy(stage, k, src, dst, device):
        return pltpu.make_async_remote_copy(
            src_ref=src, dst_ref=dst, send_sem=s_sem.at[stage, k % SLOTS], recv_sem=r_sem.at[stage, k],
            device_id=device, device_id_type=pl.DeviceIdType.MESH)

    def stage_copy(stage, k):
        if stage == 0:
            return rcopy(0, k, send_c.at[k % SLOTS], recv_c.at[k], partner)
        if stage == 1:
            return rcopy(1, k, own.at[k, pl.ds(2, 2)], recv_1.at[k], neighbour(k, 0))
        if stage == 2:
            return rcopy(2, k, own.at[k, 1], recv_2.at[k], neighbour(k, 1))
        if stage == 3:
            return rcopy(3, k, own.at[k, 0, pl.ds((1 - z0) * rh, rh)], recv_z1.at[k], z_near)
        if stage == 4:
            return rcopy(4, k, own.at[k, 0, pl.ds(z0 * rh + (1 - z1) * rq, rq)], recv_z2.at[k], z_far)
        if stage == 5:
            mine = pl.ds(z0 * rh + z1 * rq, rq)
            return rcopy(5, k, res.at[k, mine], res.at[k, mine], z_far)
        mine = pl.ds(z0 * rh, rh)
        return rcopy(6, k, res.at[k, mine], res.at[k, mine], z_near)

    def send(stage, k):
        stage_copy(stage, k).start()

    def free_slot(stage, k):
        @pl.when(k >= SLOTS)
        def _():
            stage_copy(stage, k - SLOTS).wait_send()

    def add(p, q):
        return (p.astype(F32) + q.astype(F32)).astype(BF16)

    def event(stage, k):
        if stage < 7:
            free_slot(stage, k)
        if stage > 0:
            stage_copy(stage - 1, k).wait_recv()
        if stage == 0:
            typ = k % 2
            g_load(k).wait()

            @pl.when(k + 2 < CHUNKS)
            def _():
                g_load(k + 2).start()

            for a in range(2):
                for b in range(2):
                    xx = (x + a + (b - a) * typ) % 2
                    yy = (y + b + (a - b) * typ) % 2
                    block = yy * 4 + xx * 2
                    send_c[k % SLOTS, 2 * a + b] = gbuf[k % 3, :, pl.ds(pl.multiple_of((block + 1 - c) * wide, wide), wide)].astype(BF16)
                    own[k, 2 * a + b] = gbuf[k % 3, :, pl.ds(pl.multiple_of((block + c) * wide, wide), wide)].astype(BF16)
        elif stage == 1:
            own[k] = add(own[k], recv_c[k])
        elif stage == 2:
            own[k, 0:2] = add(own[k, 0:2], recv_1[k])
        elif stage == 3:
            own[k, 0] = add(own[k, 0], recv_2[k])
        elif stage == 4:
            at = pl.ds(pl.multiple_of(z0 * rh, rh), rh)
            own[k, 0, at] = add(own[k, 0, at], recv_z1[k])
        elif stage == 5:
            at = pl.ds(pl.multiple_of(z0 * rh + z1 * rq, rq), rq)
            res[k, at] = add(own[k, 0, at], recv_z2[k])
        if stage < 7:
            send(stage, k)

    def reduce_events(u):
        for stage in range(7, -1, -1):
            k = u - FIRST - LAGS[stage]

            @pl.when((k >= 0) & (k < CHUNKS))
            def _(stage=stage, k=k):
                event(stage, k)

    def weight_events(u):
        @pl.when((u == FWD_XY) & (act == 1))
        def _():
            for p in range(4):
                wwait(2, p)
                wwait(3, p)
                for cp in fwd_xy(p):
                    cp.start()

        @pl.when((u == FWD_D) & (act == 1))
        def _():
            for p in range(4):
                wwait(4, p)
                for cp in fwd_d(p):
                    cp.start()

        for i, when in enumerate(PASS):
            @pl.when((u == when) & (act == 0))
            def _(i=i):
                for p in range(4):
                    wwait(2 + i, p)
                    wcopy(2 + i, 5 + i, p, 3 + i, partner).start()

    def slot_of(i):
        return jnp.where(i < 2, i, 2 + (i + 1 + 3 * (1 - act) + 3) % 6)

    def column_of(slot):
        b = jnp.where(slot < 5, slot, slot - 3)
        dc = jnp.where((slot == 1) | (slot >= 5), 1, 0)
        ddx = jnp.where((b == 2) | (b == 4), 1, 0)
        ddy = jnp.where((b == 3) | (b == 4), 1, 0)
        return ((y + ddy) % 2) * 4 + ((x + ddx) % 2) * 2 + (c + dc) % 2

    def dw_copy(i):
        at = pl.ds(pl.multiple_of(column_of(slot_of(i)) * wide, wide), wide)
        return pltpu.make_async_copy(dwacc.at[i % 2], dw_out.at[:, :, at], dw_sem.at[i % 2])

    def dx_copy(m):
        at = pl.ds(pl.multiple_of(m * tile, tile), tile)
        return pltpu.make_async_copy(xv.at[at], dx_out.at[at], out_sem.at[m])

    def compute(u):
        i, m = u // TILES, u % TILES
        slot = slot_of(i)
        d = i % 2
        at = pl.ds(pl.multiple_of(m * tile, tile), tile)

        @pl.when((m == 0) & ((slot == 1) | (slot >= 5)))
        def _():
            for p in range(4):
                wwait(slot, p)

        @pl.when((m == 0) & (i >= 2))
        def _():
            dw_copy(i - 2).wait()

        @pl.when(i == 0)
        def _():
            xt[m] = xv[at].T
            dyt[m] = dyv[at].T

        dot = functools.partial(lax.dot_general, preferred_element_type=F32)
        a = jnp.dot(xv[at], w1[slot], preferred_element_type=F32)
        b = jnp.dot(xv[at], w3[slot], preferred_element_type=F32)
        dh = dot(dyv[at], w2[slot], LAST)
        s = jax.nn.sigmoid(a)
        silu = a * s
        h = (silu * b).astype(BF16)
        da = (dh * b * s * (1.0 + a * (1.0 - s))).astype(BF16)
        db = (dh * silu).astype(BF16)
        dx = dot(da, w1[slot], LAST) + dot(db, w3[slot], LAST)
        dxacc[at] = jnp.where(i == 0, 0.0, dxacc[at]) + dx
        for n, (left, right) in enumerate(((xt, da), (xt, db), (dyt, h))):
            dwacc[d, n] = jnp.where(m == 0, 0.0, dwacc[d, n]) + jnp.dot(left[m], right, preferred_element_type=F32)

        @pl.when(m == TILES - 1)
        def _():
            dw_copy(i).start()

        @pl.when(i == BLOCKS - 1)
        def _():
            xv[at] = dxacc[at].astype(BF16)
            dx_copy(m).start()

    def body(u, carry):
        weight_events(u)
        reduce_events(u)
        compute(u)
        return carry

    def tail(u, carry):
        reduce_events(u)
        return carry

    lax.fori_loop(0, UNITS, body, 0)
    lax.fori_loop(UNITS, FIRST + CHUNKS + LAGS[-1], tail, 0)

    store = pltpu.make_async_copy(res, dn_out, ld_sem.at[0])
    store.start()

    for cp in own_copies():
        cp.wait_send()

    @pl.when(act == 1)
    def _():
        for cp in own_far():
            cp.wait_send()
        for p in range(4):
            for cp in fwd_xy(p) + fwd_d(p):
                cp.wait_send()

    @pl.when(act == 0)
    def _():
        for i in range(3):
            for p in range(4):
                wcopy(2 + i, 5 + i, p, 3 + i, partner).wait_send()

    for stage in range(7):
        for k in range(CHUNKS - SLOTS, CHUNKS):
            stage_copy(stage, k).wait_send()
    dw_copy(BLOCKS - 2).wait()
    dw_copy(BLOCKS - 1).wait()
    for m in range(TILES):
        dx_copy(m).wait()
    store.wait()


def solution(mesh):
    def per_device(x_blk, dy_blk, gate, up, down, g_part):
        tokens, dim = x_blk.shape
        wide = gate.shape[1]
        hidden = wide * BLOCKS
        rows = 3 * dim // CHUNKS
        tile = tokens // TILES
        g = g_part.reshape(CHUNKS, rows, hidden)
        vm = pltpu.VMEM
        dma = pltpu.SemaphoreType.DMA
        dx, dn, dw = pl.pallas_call(
            whole_step,
            out_shape=[
                jax.ShapeDtypeStruct((tokens, dim), BF16),
                jax.ShapeDtypeStruct((CHUNKS, rows, wide), BF16),
                jax.ShapeDtypeStruct((3, dim, hidden), F32),
            ],
            in_specs=[pl.BlockSpec(memory_space=pl.ANY)] * 6,
            out_specs=[pl.BlockSpec(memory_space=pl.ANY)] * 3,
            scratch_shapes=[
                vm((tokens, dim), BF16), vm((tokens, dim), BF16),
                vm((TILES, dim, tile), BF16), vm((TILES, dim, tile), BF16),
                vm((BLOCKS, dim, wide), BF16), vm((BLOCKS, dim, wide), BF16), vm((BLOCKS, wide, dim), BF16),
                vm((tokens, dim), F32), vm((2, 3, dim, wide), F32),
                vm((3, rows, hidden), F32),
                vm((SLOTS, 4, rows, wide), BF16), vm((CHUNKS, 4, rows, wide), BF16), vm((CHUNKS, 4, rows, wide), BF16),
                vm((CHUNKS, 2, rows, wide), BF16), vm((CHUNKS, rows, wide), BF16),
                vm((CHUNKS, rows // 2, wide), BF16), vm((CHUNKS, rows // 4, wide), BF16), vm((CHUNKS, rows, wide), BF16),
                dma((5,)), dma((3,)), dma((10, 4)), dma((BLOCKS, 4)), dma((7, SLOTS)), dma((7, CHUNKS)), dma((2,)), dma((TILES,)),
            ],
            compiler_params=pltpu.CompilerParams(collective_id=0, has_side_effects=True, vmem_limit_bytes=67043328),
            cost_estimate=pl.CostEstimate(flops=16 * tokens * dim * hidden, bytes_accessed=60 << 20, transcendentals=tokens * hidden),
        )(x_blk, dy_blk, gate, up, down, g)
        return dx, dn.reshape(3, dim, wide).astype(F32), dw[None]

    return jax.shard_map(
        per_device,
        mesh=mesh,
        in_specs=(P(ALL_AXES, None), P(ALL_AXES, None), P(None, GROUP_AXES), P(None, GROUP_AXES), P(GROUP_AXES, None), P(ALL_AXES, None, None, None)),
        out_specs=(P(ALL_AXES, None), P(None, None, GROUP_AXES), P(ALL_AXES, None, None, None)),
        check_vma=False,
    )
```

time: 261 us -> 140 us (0.54)
  Pallas kernels: 0 us -> 121 us
  matrix products: 105 us -> 0 us
  waiting for transfers between devices: 99.7 us -> 0 us
  other arithmetic: 22.4 us -> 3.03 us
  between operations: 13.8 us -> 0.65 us
  local copies, waits for them, and re-layouts: 18.7 us -> 14.7 us
    pallas_call x0 -> x1, Pallas kernels: none -> 121 us  [per_device(): pl.pallas_call(whole_step, out_shape=[jax.ShapeDtypeStruct((tokens, dim),...]
    dot_general x8 -> x0, matrix products: 105 us -> none  [the longest x1 24.1 us: local_backward(): lax.dot_general(dy_blk, w_down, CONTRACT_LAST, preferred_element_type=jnp...]
    all_gather x3 -> x0, waiting for transfers between devices: 70.8 us -> none  [the longest x1 25.5 us: per_device(): w_gate = lax.all_gather(gate_shard, GROUP_AXES, axis=1, tiled=True)]
    psum x1 -> x0, waiting for transfers between devices: 20.4 us -> none  [per_device(): g_summed = lax.psum(g_part[0].astype(jnp.bfloat16), 'dp')]
    convert_element_type x2 -> x1, other arithmetic: 12.9 us -> 3.03 us  [per_device(): return (dx, dn.reshape(3, dim, wide).astype(F32), dw[None])]
    broadcast_in_dim x1 -> x0, other arithmetic: 9.42 us -> none  [per_device(): return (dx_blk, g_shard.astype(jnp.float32), dw_local[None])]
    reduce_scatter x1 -> x0, waiting for transfers between devices: 6.45 us -> none  [per_device(): lax.psum_scatter(g_summed, GROUP_AXES, scatter_dimension=2, tiled=True)]
    unnamed x13 -> x4, local copies, waits for them, and re-layouts: 18.7 us -> 14.7 us
  transfers between devices with their start and end apart: 5 -> 0, of which waited for: 5 -> 0; matrix products, arithmetic and copies ran while one was open for 55% -> 0% of each run, Pallas kernels for 0% -> 0%
where the time goes in v1:
time: 140 us
  Pallas kernels  121 us (86%)
  local copies, waits for them, and re-layouts  14.7 us (10%)
  other arithmetic  3.03 us (2%)
    pallas_call x1, Pallas kernels, per_device(): pl.pallas_call(whole_step, out_shape=[jax.ShapeDtypeStruct((tokens, dim),...  121 us
    unnamed x4, local copies, waits for them, and re-layouts  14.7 us
    convert_element_type x1, other arithmetic, per_device(): return (dx, dn.reshape(3, dim, wide).astype(F32), dw[None])  3.03 us

profile of v1, /device:TPU:0, one launch (start us, length us, event | category | flops | bytes accessed | tf_op | source)
XLA Modules:
  0.0 139.6 jit_solution(15719690119080946746)
XLA Ops:
  0.6 121.3 %shard_map.85 = (bf16[2048,768]{1,0:T(8,128)(2,1)}, bf16[18,128,256]{2,1,0:T(8,128)(2,1)}, f32[3,768,2048]{2,1,0:T(8,128)}) custom-call(bf16[2048,768]{1,0:T(8,128)(2,1)} %x_hbm.1, bf16[2048,768]{1,0:T(8,128)(2,1)} %dy_hbm.1, bf16[768,256]{1,0:T(8,128)(2,1)} %wg_hbm.1, bf16[768,256]{1,0:T(8,128)(2,1)} %wu_hbm.1, bf16[256,768]{1,0:T(8,128)(2,1)} %wd_hbm.1, ...), custom_call_target="tpu_custom_call" | custom-call | flops 51539607552 | bytes 62914560 | tf_op jit(solution)/shard_map/pallas_call | solution.py:325
  121.9 0.0 copy-start
  121.9 3.0 %bitcast_convert_fusion = f32[3,768,256]{2,1,0:T(8,128)} fusion(bf16[3,768,256]{2,1,0:T(8,128)(2,1)} %bitcast.7), kind=kLoop, calls=%fused_computation | loop fusion | flops 589824 | bytes 3538944 | tf_op jit(solution)/shard_map/convert_element_type | solution.py:348
  125.0 0.0 copy-done
  125.0 1.7 %copy.11 = bf16[2048,768]{1,0:T(8,128)(2,1)} copy(bf16[2048,768]{1,0:T(8,128)(2,1)S(1)} %copy-done) | data formatting | bytes 6291456
  126.6 13.0 %copy.12 = f32[1,3,768,2048]{3,2,1,0:T(8,128)} copy(f32[1,3,768,2048]{3,2,1,0:T(8,128)} %bitcast.6) | data formatting | bytes 37748736
Async XLA Ops:
  121.9 3.0 %copy-start = (bf16[2048,768]{1,0:T(8,128)(2,1)S(1)}, bf16[2048,768]{1,0:T(8,128)(2,1)}, u32[]{:S(2)}) copy-start(bf16[2048,768]{1,0:T(8,128)(2,1)} %get-tuple-element.12) | copy-start | bytes 9437188

commit v2 on v1

--- a/solution.py
+++ b/solution.py
@@ -17,9 +17,11 @@
 UNITS = BLOCKS * TILES
 CHUNKS = 18
 FIRST = 4
-LAGS = (0, 1, 3, 5, 7, 9, 11, 13)
-FWD_XY, FWD_D = 6, 12
-PASS = (13, 19, 25)
+LAGS = (0, 1, 3, 5, 8, 10, 12)
+TAKE_XY, TAKE_D = (2, 4, 4, 6), (9, 9, 11, 15)
+Z_X, Z_Y, Z_D = (2, 4, 4, 6), (5, 8, 11, 12), (10, 11, 13, 17)
+PASS = ((9, 9, 13, 17), (14, 15, 18, 21), (17, 17, 21, 22))
+GROUP = 4
 SLOTS = 4
 
 
@@ -83,14 +85,33 @@
     def own_far():
         return [wcopy(0, s, p, i, d) for p in range(4) for s, i, d in ((2, 1, x_nbr), (3, 2, y_nbr))]
 
-    def fwd_xy(p):
-        near = [wcopy(2, 2, p, 3, z_near), wcopy(3, 3, p, 4, z_near), wcopy(2, 5, p, 5, partner), wcopy(3, 6, p, 6, partner)]
-        if p % 2 == 0:
-            return [wcopy(2, 4, p, 7, y_nbr)] + near
-        return [wcopy(3, 4, p, 7, x_nbr)] + near
-
-    def fwd_d(p):
-        return [wcopy(4, 4, p, 8, z_near), wcopy(4, 7, p, 9, partner)]
+    def z_x(p):
+        return wcopy(2, 2, p, 3, z_near)
+
+    def z_y(p):
+        return wcopy(3, 3, p, 4, z_near)
+
+    def z_d(p):
+        return wcopy(4, 4, p, 8, z_near)
+
+    def take_xy(p):
+        diagonal = wcopy(2, 4, p, 7, y_nbr) if p % 2 == 0 else wcopy(3, 4, p, 7, x_nbr)
+        return [diagonal, wcopy(2, 5, p, 5, partner), wcopy(3, 6, p, 6, partner)]
+
+    def take_d(p):
+        return wcopy(4, 7, p, 9, partner)
+
+    def pass_on(i, p):
+        return wcopy(2 + i, 5 + i, p, 3 + i, partner)
+
+    fetch, relay = {}, {}
+    for p in range(4):
+        fetch.setdefault(TAKE_XY[p], []).append(((2, 3), functools.partial(take_xy, p), p))
+        fetch.setdefault(TAKE_D[p], []).append(((4,), lambda p=p: [take_d(p)], p))
+        for units, make in ((Z_X, z_x), (Z_Y, z_y), (Z_D, z_d)):
+            fetch.setdefault(units[p], []).append(((), lambda p=p, make=make: [make(p)], p))
+        for i in range(3):
+            relay.setdefault(PASS[i][p], []).append(((2 + i,), lambda p=p, i=i: [pass_on(i, p)], p))
 
     for cp in own_loads:
         cp.wait()
@@ -143,8 +164,7 @@
         return (p.astype(F32) + q.astype(F32)).astype(BF16)
 
     def event(stage, k):
-        if stage < 7:
-            free_slot(stage, k)
+        free_slot(stage, k)
         if stage > 0:
             stage_copy(stage - 1, k).wait_recv()
         if stage == 0:
@@ -174,11 +194,10 @@
         elif stage == 5:
             at = pl.ds(pl.multiple_of(z0 * rh + z1 * rq, rq), rq)
             res[k, at] = add(own[k, 0, at], recv_z2[k])
-        if stage < 7:
-            send(stage, k)
+        send(stage, k)
 
     def reduce_events(u):
-        for stage in range(7, -1, -1):
+        for stage in range(6, -1, -1):
             k = u - FIRST - LAGS[stage]
 
             @pl.when((k >= 0) & (k < CHUNKS))
@@ -186,27 +205,18 @@
                 event(stage, k)
 
     def weight_events(u):
-        @pl.when((u == FWD_XY) & (act == 1))
-        def _():
-            for p in range(4):
-                wwait(2, p)
-                wwait(3, p)
-                for cp in fwd_xy(p):
-                    cp.start()
-
-        @pl.when((u == FWD_D) & (act == 1))
-        def _():
-            for p in range(4):
-                wwait(4, p)
-                for cp in fwd_d(p):
-                    cp.start()
-
-        for i, when in enumerate(PASS):
-            @pl.when((u == when) & (act == 0))
-            def _(i=i):
-                for p in range(4):
-                    wwait(2 + i, p)
-                    wcopy(2 + i, 5 + i, p, 3 + i, partner).start()
+        for mine, table in ((1, fetch), (0, relay)):
+            for group in sorted({t // GROUP for t in table}):
+                @pl.when((u // GROUP == group) & (act == mine))
+                def _(table=table, group=group):
+                    for t in sorted(t for t in table if t // GROUP == group):
+                        @pl.when(u == t)
+                        def _(t=t):
+                            for slots, make, p in table[t]:
+                                for slot in slots:
+                                    wwait(slot, p)
+                                for cp in make():
+                                    cp.start()
 
     def slot_of(i):
         return jnp.where(i < 2, i, 2 + (i + 1 + 3 * (1 - act) + 3) % 6)
@@ -282,6 +292,8 @@
     lax.fori_loop(0, UNITS, body, 0)
     lax.fori_loop(UNITS, FIRST + CHUNKS + LAGS[-1], tail, 0)
 
+    for k in range(CHUNKS):
+        stage_copy(6, k).wait_recv()
     store = pltpu.make_async_copy(res, dn_out, ld_sem.at[0])
     store.start()
 
@@ -293,14 +305,14 @@
         for cp in own_far():
             cp.wait_send()
         for p in range(4):
-            for cp in fwd_xy(p) + fwd_d(p):
+            for cp in take_xy(p) + [take_d(p), z_x(p), z_y(p), z_d(p)]:
                 cp.wait_send()
 
     @pl.when(act == 0)
     def _():
         for i in range(3):
             for p in range(4):
-                wcopy(2 + i, 5 + i, p, 3 + i, partner).wait_send()
+                pass_on(i, p).wait_send()
 
     for stage in range(7):
         for k in range(CHUNKS - SLOTS, CHUNKS):

time: 140 us -> 128 us (0.914)
  Pallas kernels: 121 us -> 110 us
    pallas_call x1, Pallas kernels: 121 us -> 110 us  [per_device(): pl.pallas_call(whole_step, out_shape=[jax.ShapeDtypeStruct((tokens, dim),...]
where the time goes in v2:
time: 128 us
  Pallas kernels  110 us (86%)
  local copies, waits for them, and re-layouts  14.7 us (11%)
  other arithmetic  3.03 us (2%)
    pallas_call x1, Pallas kernels, per_device(): pl.pallas_call(whole_step, out_shape=[jax.ShapeDtypeStruct((tokens, dim),...  110 us
    unnamed x4, local copies, waits for them, and re-layouts  14.7 us
    convert_element_type x1, other arithmetic, per_device(): return (dx, dn.reshape(3, dim, wide).astype(F32), dw[None])  3.03 us

profile of v2, /device:TPU:0, one launch (start us, length us, event | category | flops | bytes accessed | tf_op | source)
XLA Modules:
  0.0 128.1 jit_solution(12543277438625873286)
XLA Ops:
  0.6 109.7 %shard_map.85 = (bf16[2048,768]{1,0:T(8,128)(2,1)}, bf16[18,128,256]{2,1,0:T(8,128)(2,1)}, f32[3,768,2048]{2,1,0:T(8,128)}) custom-call(bf16[2048,768]{1,0:T(8,128)(2,1)} %x_hbm.1, bf16[2048,768]{1,0:T(8,128)(2,1)} %dy_hbm.1, bf16[768,256]{1,0:T(8,128)(2,1)} %wg_hbm.1, bf16[768,256]{1,0:T(8,128)(2,1)} %wu_hbm.1, bf16[256,768]{1,0:T(8,128)(2,1)} %wd_hbm.1, ...), custom_call_target="tpu_custom_call" | custom-call | flops 51539607552 | bytes 62914560 | tf_op jit(solution)/shard_map/pallas_call | solution.py:337
  110.4 0.0 copy-start
  110.4 3.0 %bitcast_convert_fusion = f32[3,768,256]{2,1,0:T(8,128)} fusion(bf16[3,768,256]{2,1,0:T(8,128)(2,1)} %bitcast.7), kind=kLoop, calls=%fused_computation | loop fusion | flops 589824 | bytes 3538944 | tf_op jit(solution)/shard_map/convert_element_type | solution.py:360
  113.4 0.0 copy-done
  113.4 1.7 %copy.11 = bf16[2048,768]{1,0:T(8,128)(2,1)} copy(bf16[2048,768]{1,0:T(8,128)(2,1)S(1)} %copy-done) | data formatting | bytes 6291456
  115.1 13.0 %copy.12 = f32[1,3,768,2048]{3,2,1,0:T(8,128)} copy(f32[1,3,768,2048]{3,2,1,0:T(8,128)} %bitcast.6) | data formatting | bytes 37748736
Async XLA Ops:
  110.4 3.0 %copy-start = (bf16[2048,768]{1,0:T(8,128)(2,1)S(1)}, bf16[2048,768]{1,0:T(8,128)(2,1)}, u32[]{:S(2)}) copy-start(bf16[2048,768]{1,0:T(8,128)(2,1)} %get-tuple-element.12) | copy-start | bytes 9437188

commit v3 on v2

--- a/solution.py
+++ b/solution.py
@@ -10,6 +10,7 @@
 ALL_AXES = ("dp", "row", "fsdp")
 GROUP_AXES = ("row", "fsdp")
 LAST = (((1,), (1,)), ((), ()))
+FIRST_TO_LAST = (((1,), (0,)), ((), ()))
 F32, BF16 = jnp.float32, jnp.bfloat16
 
 BLOCKS = 8
@@ -26,7 +27,7 @@
 
 
 def whole_step(x_hbm, dy_hbm, wg_hbm, wu_hbm, wd_hbm, g_hbm, dx_out, dn_out, dw_out,
-               xv, dyv, xt, dyt, w1, w3, w2, dxacc, dwacc,
+               xv, dyv, xt, dyt, w13, w2, dab_even, dab_odd, h_even, h_odd, dxacc, dwacc,
                gbuf, send_c, own, recv_c, recv_1, recv_2, recv_z1, recv_z2, res,
                ld_sem, g_sem, ws_sem, wr_sem, s_sem, r_sem, dw_sem, out_sem):
     z, y, f = lax.axis_index("dp"), lax.axis_index("row"), lax.axis_index("fsdp")
@@ -34,7 +35,7 @@
     z0, z1 = z % 2, z // 2
     act = (z0 + c + 1) % 2
     tile = xv.shape[0] // TILES
-    wide = w1.shape[2]
+    wide = w13.shape[2] // 2
     half_w2 = w2.shape[1] // 2
     rows = gbuf.shape[1]
     rh, rq = rows // 2, rows // 4
@@ -48,7 +49,7 @@
     z_near = dev(dz=z + 1 - 2 * z0)
     z_far = dev(dz=(z + 2) % 4)
 
-    own_loads = [pltpu.make_async_copy(s, d.at[0], ld_sem.at[i]) for i, (s, d) in enumerate(((wg_hbm, w1), (wu_hbm, w3), (wd_hbm, w2)))]
+    own_loads = [pltpu.make_async_copy(s, d, ld_sem.at[i]) for i, (s, d) in enumerate(((wg_hbm, w13.at[0, :, pl.ds(0, wide)]), (wu_hbm, w13.at[0, :, pl.ds(wide, wide)]), (wd_hbm, w2.at[0])))]
     act_loads = [pltpu.make_async_copy(s, d, ld_sem.at[3 + i]) for i, (s, d) in enumerate(((x_hbm, xv), (dy_hbm, dyv)))]
     for cp in own_loads + act_loads:
         cp.start()
@@ -65,10 +66,8 @@
     pl.semaphore_wait(barrier, 5)
 
     def part(slot, p):
-        if p == 0:
-            return w1.at[slot]
-        if p == 1:
-            return w3.at[slot]
+        if p < 2:
+            return w13.at[slot, :, pl.ds(p * wide, wide)]
         return w2.at[slot, pl.ds((p - 2) * half_w2, half_w2)]
 
     def wcopy(src, dst, p, sem, device):
@@ -236,39 +235,65 @@
         at = pl.ds(pl.multiple_of(m * tile, tile), tile)
         return pltpu.make_async_copy(xv.at[at], dx_out.at[at], out_sem.at[m])
 
-    def compute(u):
+    dot = functools.partial(lax.dot_general, preferred_element_type=F32)
+
+    def rows_of(m):
+        return pl.ds(pl.multiple_of(m * tile, tile), tile)
+
+    def before(u):
+        weight_events(u)
+        reduce_events(u)
         i, m = u // TILES, u % TILES
         slot = slot_of(i)
-        d = i % 2
-        at = pl.ds(pl.multiple_of(m * tile, tile), tile)
 
         @pl.when((m == 0) & ((slot == 1) | (slot >= 5)))
         def _():
             for p in range(4):
                 wwait(slot, p)
 
-        @pl.when((m == 0) & (i >= 2))
+        @pl.when(i == 0)
+        def _():
+            xt[m] = xv[rows_of(m)].T
+            dyt[m] = dyv[rows_of(m)].T
+
+        @pl.when((m == 1) & (i >= 2))
         def _():
             dw_copy(i - 2).wait()
 
-        @pl.when(i == 0)
-        def _():
-            xt[m] = xv[at].T
-            dyt[m] = dyv[at].T
-
-        dot = functools.partial(lax.dot_general, preferred_element_type=F32)
-        a = jnp.dot(xv[at], w1[slot], preferred_element_type=F32)
-        b = jnp.dot(xv[at], w3[slot], preferred_element_type=F32)
-        dh = dot(dyv[at], w2[slot], LAST)
+    def products(u):
+        slot, at = slot_of(u // TILES), rows_of(u % TILES)
+        half = tile // 2
+        first = pl.multiple_of((u % TILES) * tile, tile)
+        dh = [dot(dyv[pl.ds(first + n * half, half)], w2[slot], LAST) for n in range(2)]
+        return dot(xv[at], w13[slot], FIRST_TO_LAST), jnp.concatenate(dh, axis=0)
+
+    def gate(ab, dh, dab, h):
+        a, b = ab[:, :wide], ab[:, wide:]
         s = jax.nn.sigmoid(a)
         silu = a * s
-        h = (silu * b).astype(BF16)
-        da = (dh * b * s * (1.0 + a * (1.0 - s))).astype(BF16)
-        db = (dh * silu).astype(BF16)
-        dx = dot(da, w1[slot], LAST) + dot(db, w3[slot], LAST)
-        dxacc[at] = jnp.where(i == 0, 0.0, dxacc[at]) + dx
-        for n, (left, right) in enumerate(((xt, da), (xt, db), (dyt, h))):
-            dwacc[d, n] = jnp.where(m == 0, 0.0, dwacc[d, n]) + jnp.dot(left[m], right, preferred_element_type=F32)
+        h[...] = (silu * b).astype(BF16)
+        dab[:, :wide] = (dh * b * s * (1.0 + a * (1.0 - s))).astype(BF16)
+        dab[:, wide:] = (dh * silu).astype(BF16)
+
+    def gradients(u, dab, h):
+        i, m = u // TILES, u % TILES
+        d = i % 2
+        half, dim = tile // 2, xt.shape[1] // 2
+        first = pl.multiple_of(m * tile, tile)
+        for n in range(2):
+            at = pl.ds(n * dim, dim)
+            dwacc[d, 2, at] = jnp.where(m == 0, 0.0, dwacc[d, 2, at]) + dot(dyt[m, at], h[...], FIRST_TO_LAST)
+        for n in range(2):
+            at = pl.ds(first + n * half, half)
+            dxacc[at] = jnp.where(i == 0, 0.0, dxacc[at]) + dot(dab[n * half:(n + 1) * half], w13[slot_of(i)], LAST)
+        for n in range(2):
+            at = pl.ds(n * dim, dim)
+            left = dot(xt[m, at], dab[...], FIRST_TO_LAST)
+            dwacc[d, 0, at] = jnp.where(m == 0, 0.0, dwacc[d, 0, at]) + left[:, :wide]
+            dwacc[d, 1, at] = jnp.where(m == 0, 0.0, dwacc[d, 1, at]) + left[:, wide:]
+
+    def after(u):
+        i, m = u // TILES, u % TILES
 
         @pl.when(m == TILES - 1)
         def _():
@@ -276,21 +301,36 @@
 
         @pl.when(i == BLOCKS - 1)
         def _():
+            at = rows_of(m)
             xv[at] = dxacc[at].astype(BF16)
             dx_copy(m).start()
 
-    def body(u, carry):
-        weight_events(u)
-        reduce_events(u)
-        compute(u)
+    even, odd = (dab_even, h_even), (dab_odd, h_odd)
+
+    def step(u, now, last):
+        before(u)
+        ab, dh = products(u)
+        gradients(u - 1, *last)
+        gate(ab, dh, *now)
+        after(u - 1)
+
+    def body(v, carry):
+        step(2 * v + 1, odd, even)
+        step(2 * v + 2, even, odd)
         return carry
 
     def tail(u, carry):
         reduce_events(u)
         return carry
 
-    lax.fori_loop(0, UNITS, body, 0)
-    lax.fori_loop(UNITS, FIRST + CHUNKS + LAGS[-1], tail, 0)
+    before(0)
+    gate(*products(0), *even)
+    lax.fori_loop(0, UNITS // 2 - 1, body, 0)
+    step(UNITS - 1, odd, even)
+    reduce_events(UNITS)
+    gradients(UNITS - 1, *odd)
+    after(UNITS - 1)
+    lax.fori_loop(UNITS + 1, FIRST + CHUNKS + LAGS[-1], tail, 0)
 
     for k in range(CHUNKS):
         stage_copy(6, k).wait_recv()
@@ -346,7 +386,8 @@
             scratch_shapes=[
                 vm((tokens, dim), BF16), vm((tokens, dim), BF16),
                 vm((TILES, dim, tile), BF16), vm((TILES, dim, tile), BF16),
-                vm((BLOCKS, dim, wide), BF16), vm((BLOCKS, dim, wide), BF16), vm((BLOCKS, wide, dim), BF16),
+                vm((BLOCKS, dim, 2 * wide), BF16), vm((BLOCKS, wide, dim), BF16),
+                vm((tile, 2 * wide), BF16), vm((tile, 2 * wide), BF16), vm((tile, wide), BF16), vm((tile, wide), BF16),
                 vm((tokens, dim), F32), vm((2, 3, dim, wide), F32),
                 vm((3, rows, hidden), F32),
                 vm((SLOTS, 4, rows, wide), BF16), vm((CHUNKS, 4, rows, wide), BF16), vm((CHUNKS, 4, rows, wide), BF16),

time: 128 us -> 123 us (0.961)
  Pallas kernels: 110 us -> 104 us
    pallas_call x1, Pallas kernels: 110 us -> 104 us  [per_device(): pl.pallas_call(whole_step, out_shape=[jax.ShapeDtypeStruct((tokens, dim),...]
where the time goes in v3:
time: 123 us
  Pallas kernels  104 us (85%)
  local copies, waits for them, and re-layouts  14.7 us (12%)
  other arithmetic  3.03 us (2%)
    pallas_call x1, Pallas kernels, per_device(): pl.pallas_call(whole_step, out_shape=[jax.ShapeDtypeStruct((tokens, dim),...  104 us
    unnamed x4, local copies, waits for them, and re-layouts  14.7 us
    convert_element_type x1, other arithmetic, per_device(): return (dx, dn.reshape(3, dim, wide).astype(F32), dw[None])  3.03 us

profile of v3, /device:TPU:0, one launch (start us, length us, event | category | flops | bytes accessed | tf_op | source)
XLA Modules:
  0.0 122.6 jit_solution(5728329115220552112)
XLA Ops:
  0.6 104.3 %shard_map.85 = (bf16[2048,768]{1,0:T(8,128)(2,1)}, bf16[18,128,256]{2,1,0:T(8,128)(2,1)}, f32[3,768,2048]{2,1,0:T(8,128)}) custom-call(bf16[2048,768]{1,0:T(8,128)(2,1)} %x_hbm.1, bf16[2048,768]{1,0:T(8,128)(2,1)} %dy_hbm.1, bf16[768,256]{1,0:T(8,128)(2,1)} %wg_hbm.1, bf16[768,256]{1,0:T(8,128)(2,1)} %wu_hbm.1, bf16[256,768]{1,0:T(8,128)(2,1)} %wd_hbm.1, ...), custom_call_target="tpu_custom_call" | custom-call | flops 51539607552 | bytes 62914560 | tf_op jit(solution)/shard_map/pallas_call | solution.py:377
  104.9 0.0 copy-start
  104.9 3.0 %bitcast_convert_fusion = f32[3,768,256]{2,1,0:T(8,128)} fusion(bf16[3,768,256]{2,1,0:T(8,128)(2,1)} %bitcast.7), kind=kLoop, calls=%fused_computation | loop fusion | flops 589824 | bytes 3538944 | tf_op jit(solution)/shard_map/convert_element_type | solution.py:401
  108.0 0.0 copy-done
  108.0 1.7 %copy.11 = bf16[2048,768]{1,0:T(8,128)(2,1)} copy(bf16[2048,768]{1,0:T(8,128)(2,1)S(1)} %copy-done) | data formatting | bytes 6291456
  109.6 13.0 %copy.12 = f32[1,3,768,2048]{3,2,1,0:T(8,128)} copy(f32[1,3,768,2048]{3,2,1,0:T(8,128)} %bitcast.6) | data formatting | bytes 37748736
Async XLA Ops:
  104.9 3.0 %copy-start = (bf16[2048,768]{1,0:T(8,128)(2,1)S(1)}, bf16[2048,768]{1,0:T(8,128)(2,1)}, u32[]{:S(2)}) copy-start(bf16[2048,768]{1,0:T(8,128)(2,1)} %get-tuple-element.12) | copy-start | bytes 9437188

commit v4 on v3

--- a/solution.py
+++ b/solution.py
@@ -17,18 +17,18 @@
 TILES = 4
 UNITS = BLOCKS * TILES
 CHUNKS = 18
-FIRST = 4
-LAGS = (0, 1, 3, 5, 8, 10, 12)
-TAKE_XY, TAKE_D = (2, 4, 4, 6), (9, 9, 11, 15)
-Z_X, Z_Y, Z_D = (2, 4, 4, 6), (5, 8, 11, 12), (10, 11, 13, 17)
-PASS = ((9, 9, 13, 17), (14, 15, 18, 21), (17, 17, 21, 22))
+FIRST = 5
+LAGS = (0, 2, 4, 6, 10)
+TAKE_XY, TAKE_D = (3, 4, 6, 6), (9, 10, 11, 14)
+Z_X, Z_Y = (3, 4, 8, 10), (4, 7, 9, 13)
+PASS_X, PASS_Y, PASS_D = (11, 13, 15, 16), (13, 14, 17, 17), (24, 25, 26, 27)
 GROUP = 4
 SLOTS = 4
 
 
 def whole_step(x_hbm, dy_hbm, wg_hbm, wu_hbm, wd_hbm, g_hbm, dx_out, dn_out, dw_out,
                xv, dyv, xt, dyt, w13, w2, dab_even, dab_odd, h_even, h_odd, dxacc, dwacc,
-               gbuf, send_c, own, recv_c, recv_1, recv_2, recv_z1, recv_z2, res,
+               gbuf, send_c, own, recv_c, recv_1, recv_2, recv_z, res,
                ld_sem, g_sem, ws_sem, wr_sem, s_sem, r_sem, dw_sem, out_sem):
     z, y, f = lax.axis_index("dp"), lax.axis_index("row"), lax.axis_index("fsdp")
     x, c = f // 2, f % 2
@@ -38,7 +38,7 @@
     wide = w13.shape[2] // 2
     half_w2 = w2.shape[1] // 2
     rows = gbuf.shape[1]
-    rh, rq = rows // 2, rows // 4
+    rq = rows // 4
 
     def dev(dz=None, yy=None, xx=None, cc=None):
         zz = z if dz is None else dz
@@ -47,7 +47,7 @@
     partner = dev(cc=1 - c)
     x_nbr, y_nbr = dev(xx=1 - x), dev(yy=1 - y)
     z_near = dev(dz=z + 1 - 2 * z0)
-    z_far = dev(dz=(z + 2) % 4)
+    others = [dev(dz=(z + j) % 4) for j in (1, 2, 3)]
 
     own_loads = [pltpu.make_async_copy(s, d, ld_sem.at[i]) for i, (s, d) in enumerate(((wg_hbm, w13.at[0, :, pl.ds(0, wide)]), (wu_hbm, w13.at[0, :, pl.ds(wide, wide)]), (wd_hbm, w2.at[0])))]
     act_loads = [pltpu.make_async_copy(s, d, ld_sem.at[3 + i]) for i, (s, d) in enumerate(((x_hbm, xv), (dy_hbm, dyv)))]
@@ -61,9 +61,9 @@
     g_load(1).start()
 
     barrier = pltpu.get_barrier_semaphore()
-    for d in (partner, x_nbr, y_nbr, z_near, z_far):
+    for d in (partner, x_nbr, y_nbr, *others):
         pl.semaphore_signal(barrier, inc=1, device_id=d, device_id_type=pl.DeviceIdType.MESH)
-    pl.semaphore_wait(barrier, 5)
+    pl.semaphore_wait(barrier, 6)
 
     def part(slot, p):
         if p < 2:
@@ -90,27 +90,25 @@
     def z_y(p):
         return wcopy(3, 3, p, 4, z_near)
 
-    def z_d(p):
-        return wcopy(4, 4, p, 8, z_near)
-
-    def take_xy(p):
-        diagonal = wcopy(2, 4, p, 7, y_nbr) if p % 2 == 0 else wcopy(3, 4, p, 7, x_nbr)
-        return [diagonal, wcopy(2, 5, p, 5, partner), wcopy(3, 6, p, 6, partner)]
+    def take_x(p):
+        return [wcopy(2, 5, p, 5, partner)] + ([wcopy(2, 4, p, 7, y_nbr)] if p % 2 == 0 else [])
+
+    def take_y(p):
+        return [wcopy(3, 6, p, 6, partner)] + ([wcopy(3, 4, p, 7, x_nbr)] if p % 2 == 1 else [])
 
     def take_d(p):
-        return wcopy(4, 7, p, 9, partner)
-
-    def pass_on(i, p):
-        return wcopy(2 + i, 5 + i, p, 3 + i, partner)
+        return [wcopy(4, 7, p, 8, partner)]
 
     fetch, relay = {}, {}
     for p in range(4):
-        fetch.setdefault(TAKE_XY[p], []).append(((2, 3), functools.partial(take_xy, p), p))
-        fetch.setdefault(TAKE_D[p], []).append(((4,), lambda p=p: [take_d(p)], p))
-        for units, make in ((Z_X, z_x), (Z_Y, z_y), (Z_D, z_d)):
-            fetch.setdefault(units[p], []).append(((), lambda p=p, make=make: [make(p)], p))
-        for i in range(3):
-            relay.setdefault(PASS[i][p], []).append(((2 + i,), lambda p=p, i=i: [pass_on(i, p)], p))
+        fetch.setdefault(TAKE_XY[p], []).append((2, functools.partial(take_x, p), p))
+        fetch.setdefault(TAKE_XY[p], []).append((3, functools.partial(take_y, p), p))
+        for units, make in ((Z_X, z_x), (Z_Y, z_y)):
+            fetch.setdefault(units[p], []).append((None, lambda p=p, make=make: [make(p)], p))
+        relay.setdefault(PASS_X[p], []).append((2, functools.partial(take_x, p), p))
+        relay.setdefault(PASS_Y[p], []).append((3, functools.partial(take_y, p), p))
+        fetch.setdefault(TAKE_D[p], []).append((4, functools.partial(take_d, p), p))
+        relay.setdefault(PASS_D[p], []).append((4, functools.partial(take_d, p), p))
 
     for cp in own_loads:
         cp.wait()
@@ -133,6 +131,9 @@
         return pltpu.make_async_remote_copy(
             src_ref=src, dst_ref=dst, send_sem=s_sem.at[stage, k % SLOTS], recv_sem=r_sem.at[stage, k],
             device_id=device, device_id_type=pl.DeviceIdType.MESH)
+
+    def quarter(zz):
+        return pl.ds(pl.multiple_of(zz % 4 * rq, rq), rq)
 
     def stage_copy(stage, k):
         if stage == 0:
@@ -141,18 +142,13 @@
             return rcopy(1, k, own.at[k, pl.ds(2, 2)], recv_1.at[k], neighbour(k, 0))
         if stage == 2:
             return rcopy(2, k, own.at[k, 1], recv_2.at[k], neighbour(k, 1))
-        if stage == 3:
-            return rcopy(3, k, own.at[k, 0, pl.ds((1 - z0) * rh, rh)], recv_z1.at[k], z_near)
-        if stage == 4:
-            return rcopy(4, k, own.at[k, 0, pl.ds(z0 * rh + (1 - z1) * rq, rq)], recv_z2.at[k], z_far)
-        if stage == 5:
-            mine = pl.ds(z0 * rh + z1 * rq, rq)
-            return rcopy(5, k, res.at[k, mine], res.at[k, mine], z_far)
-        mine = pl.ds(z0 * rh, rh)
-        return rcopy(6, k, res.at[k, mine], res.at[k, mine], z_near)
-
-    def send(stage, k):
-        stage_copy(stage, k).start()
+        if stage < 6:
+            j = stage - 3
+            return rcopy(stage, k, own.at[k, 0, quarter(z + j + 1)], recv_z.at[k, j], others[j])
+        return rcopy(stage, k, res.at[k, quarter(z)], res.at[k, quarter(z)], others[stage - 6])
+
+    STARTS = ((0,), (1,), (2,), (3, 4, 5), (6, 7, 8))
+    NEEDS = ((), (0,), (1,), (2,), (3, 4, 5))
 
     def free_slot(stage, k):
         @pl.when(k >= SLOTS)
@@ -163,9 +159,10 @@
         return (p.astype(F32) + q.astype(F32)).astype(BF16)
 
     def event(stage, k):
-        free_slot(stage, k)
-        if stage > 0:
-            stage_copy(stage - 1, k).wait_recv()
+        for n in STARTS[stage]:
+            free_slot(n, k)
+        for n in NEEDS[stage]:
+            stage_copy(n, k).wait_recv()
         if stage == 0:
             typ = k % 2
             g_load(k).wait()
@@ -187,16 +184,16 @@
             own[k, 0:2] = add(own[k, 0:2], recv_1[k])
         elif stage == 3:
             own[k, 0] = add(own[k, 0], recv_2[k])
-        elif stage == 4:
-            at = pl.ds(pl.multiple_of(z0 * rh, rh), rh)
-            own[k, 0, at] = add(own[k, 0, at], recv_z1[k])
-        elif stage == 5:
-            at = pl.ds(pl.multiple_of(z0 * rh + z1 * rq, rq), rq)
-            res[k, at] = add(own[k, 0, at], recv_z2[k])
-        send(stage, k)
+        else:
+            total = own[k, 0, quarter(z)].astype(F32)
+            for j in range(3):
+                total += recv_z[k, j].astype(F32)
+            res[k, quarter(z)] = total.astype(BF16)
+        for n in STARTS[stage]:
+            stage_copy(n, k).start()
 
     def reduce_events(u):
-        for stage in range(6, -1, -1):
+        for stage in range(4, -1, -1):
             k = u - FIRST - LAGS[stage]
 
             @pl.when((k >= 0) & (k < CHUNKS))
@@ -211,8 +208,8 @@
                     for t in sorted(t for t in table if t // GROUP == group):
                         @pl.when(u == t)
                         def _(t=t):
-                            for slots, make, p in table[t]:
-                                for slot in slots:
+                            for slot, make, p in table[t]:
+                                if slot is not None:
                                     wwait(slot, p)
                                 for cp in make():
                                     cp.start()
@@ -333,7 +330,8 @@
     lax.fori_loop(UNITS + 1, FIRST + CHUNKS + LAGS[-1], tail, 0)
 
     for k in range(CHUNKS):
-        stage_copy(6, k).wait_recv()
+        for n in (6, 7, 8):
+            stage_copy(n, k).wait_recv()
     store = pltpu.make_async_copy(res, dn_out, ld_sem.at[0])
     store.start()
 
@@ -345,16 +343,13 @@
         for cp in own_far():
             cp.wait_send()
         for p in range(4):
-            for cp in take_xy(p) + [take_d(p), z_x(p), z_y(p), z_d(p)]:
-                cp.wait_send()
-
-    @pl.when(act == 0)
-    def _():
-        for i in range(3):
-            for p in range(4):
-                pass_on(i, p).wait_send()
-
-    for stage in range(7):
+            z_x(p).wait_send()
+            z_y(p).wait_send()
+
+    for p in range(4):
+        for cp in take_x(p) + take_y(p) + take_d(p):
+            cp.wait_send()
+    for stage in range(9):
         for k in range(CHUNKS - SLOTS, CHUNKS):
             stage_copy(stage, k).wait_send()
     dw_copy(BLOCKS - 2).wait()
@@ -392,8 +387,8 @@
                 vm((3, rows, hidden), F32),
                 vm((SLOTS, 4, rows, wide), BF16), vm((CHUNKS, 4, rows, wide), BF16), vm((CHUNKS, 4, rows, wide), BF16),
                 vm((CHUNKS, 2, rows, wide), BF16), vm((CHUNKS, rows, wide), BF16),
-                vm((CHUNKS, rows // 2, wide), BF16), vm((CHUNKS, rows // 4, wide), BF16), vm((CHUNKS, rows, wide), BF16),
-                dma((5,)), dma((3,)), dma((10, 4)), dma((BLOCKS, 4)), dma((7, SLOTS)), dma((7, CHUNKS)), dma((2,)), dma((TILES,)),
+                vm((CHUNKS, 3, rows // 4, wide), BF16), vm((CHUNKS, rows, wide), BF16),
+                dma((5,)), dma((3,)), dma((10, 4)), dma((BLOCKS, 4)), dma((9, SLOTS)), dma((9, CHUNKS)), dma((2,)), dma((TILES,)),
             ],
             compiler_params=pltpu.CompilerParams(collective_id=0, has_side_effects=True, vmem_limit_bytes=67043328),
             cost_estimate=pl.CostEstimate(flops=16 * tokens * dim * hidden, bytes_accessed=60 << 20, transcendentals=tokens * hidden),

time: 123 us -> 121 us (0.984)
    pallas_call x1, Pallas kernels: 104 us -> 103 us  [per_device(): pl.pallas_call(whole_step, out_shape=[jax.ShapeDtypeStruct((tokens, dim),...]
where the time goes in v4:
time: 121 us
  Pallas kernels  103 us (85%)
  local copies, waits for them, and re-layouts  14.7 us (12%)
  other arithmetic  3.03 us (3%)
    pallas_call x1, Pallas kernels, per_device(): pl.pallas_call(whole_step, out_shape=[jax.ShapeDtypeStruct((tokens, dim),...  103 us
    unnamed x4, local copies, waits for them, and re-layouts  14.7 us
    convert_element_type x1, other arithmetic, per_device(): return (dx, dn.reshape(3, dim, wide).astype(F32), dw[None])  3.03 us

profile of v4, /device:TPU:0, one launch (start us, length us, event | category | flops | bytes accessed | tf_op | source)
XLA Modules:
  0.0 121.0 jit_solution(215755009744882923)
XLA Ops:
  0.6 102.7 %shard_map.85 = (bf16[2048,768]{1,0:T(8,128)(2,1)}, bf16[18,128,256]{2,1,0:T(8,128)(2,1)}, f32[3,768,2048]{2,1,0:T(8,128)}) custom-call(bf16[2048,768]{1,0:T(8,128)(2,1)} %x_hbm.1, bf16[2048,768]{1,0:T(8,128)(2,1)} %dy_hbm.1, bf16[768,256]{1,0:T(8,128)(2,1)} %wg_hbm.1, bf16[768,256]{1,0:T(8,128)(2,1)} %wu_hbm.1, bf16[256,768]{1,0:T(8,128)(2,1)} %wd_hbm.1, ...), custom_call_target="tpu_custom_call" | custom-call | flops 51539607552 | bytes 62914560 | tf_op jit(solution)/shard_map/pallas_call | solution.py:372
  103.3 0.0 copy-start
  103.3 3.0 %bitcast_convert_fusion = f32[3,768,256]{2,1,0:T(8,128)} fusion(bf16[3,768,256]{2,1,0:T(8,128)(2,1)} %bitcast.7), kind=kLoop, calls=%fused_computation | loop fusion | flops 589824 | bytes 3538944 | tf_op jit(solution)/shard_map/convert_element_type | solution.py:396
  106.4 0.0 copy-done
  106.4 1.7 %copy.11 = bf16[2048,768]{1,0:T(8,128)(2,1)} copy(bf16[2048,768]{1,0:T(8,128)(2,1)S(1)} %copy-done) | data formatting | bytes 6291456
  108.0 13.0 %copy.12 = f32[1,3,768,2048]{3,2,1,0:T(8,128)} copy(f32[1,3,768,2048]{3,2,1,0:T(8,128)} %bitcast.6) | data formatting | bytes 37748736
Async XLA Ops:
  103.3 3.0 %copy-start = (bf16[2048,768]{1,0:T(8,128)(2,1)S(1)}, bf16[2048,768]{1,0:T(8,128)(2,1)}, u32[]{:S(2)}) copy-start(bf16[2048,768]{1,0:T(8,128)(2,1)} %get-tuple-element.12) | copy-start | bytes 9437188

commit v5 on v4

--- a/solution.py
+++ b/solution.py
@@ -17,28 +17,29 @@
 TILES = 4
 UNITS = BLOCKS * TILES
 CHUNKS = 18
-FIRST = 5
-LAGS = (0, 2, 4, 6, 10)
-TAKE_XY, TAKE_D = (3, 4, 6, 6), (9, 10, 11, 14)
-Z_X, Z_Y = (3, 4, 8, 10), (4, 7, 9, 13)
-PASS_X, PASS_Y, PASS_D = (11, 13, 15, 16), (13, 14, 17, 17), (24, 25, 26, 27)
+FIRST = 1
+LAGS = (0, 1, 4, 7, 11, 13, 15)
+TAKE_XY, TAKE_D = (2, 3, 4, 6), (10, 11, 14, 14)
+Z_X, Z_Y = (2, 3, 4, 6), (4, 6, 10, 15)
+PASS_X, PASS_Y, PASS_D = (10, 10, 13, 13), (14, 14, 16, 17), (22, 25, 27, 27)
 GROUP = 4
 SLOTS = 4
 
 
 def whole_step(x_hbm, dy_hbm, wg_hbm, wu_hbm, wd_hbm, g_hbm, dx_out, dn_out, dw_out,
                xv, dyv, xt, dyt, w13, w2, dab_even, dab_odd, h_even, h_odd, dxacc, dwacc,
-               gbuf, send_c, own, recv_c, recv_1, recv_2, recv_z, res,
+               gbuf, send_c, own, recv_c, recv_1, recv_2, recv_z1, recv_z2, res,
                ld_sem, g_sem, ws_sem, wr_sem, s_sem, r_sem, dw_sem, out_sem):
     z, y, f = lax.axis_index("dp"), lax.axis_index("row"), lax.axis_index("fsdp")
     x, c = f // 2, f % 2
-    z0, z1 = z % 2, z // 2
+    z0 = z % 2
     act = (z0 + c + 1) % 2
     tile = xv.shape[0] // TILES
     wide = w13.shape[2] // 2
     half_w2 = w2.shape[1] // 2
     rows = gbuf.shape[1]
-    rq = rows // 4
+    rh = rows // 2
+    inner = (z + 1) // 2 % 2
 
     def dev(dz=None, yy=None, xx=None, cc=None):
         zz = z if dz is None else dz
@@ -47,7 +48,7 @@
     partner = dev(cc=1 - c)
     x_nbr, y_nbr = dev(xx=1 - x), dev(yy=1 - y)
     z_near = dev(dz=z + 1 - 2 * z0)
-    others = [dev(dz=(z + j) % 4) for j in (1, 2, 3)]
+    z_mirror = dev(dz=3 - z)
 
     own_loads = [pltpu.make_async_copy(s, d, ld_sem.at[i]) for i, (s, d) in enumerate(((wg_hbm, w13.at[0, :, pl.ds(0, wide)]), (wu_hbm, w13.at[0, :, pl.ds(wide, wide)]), (wd_hbm, w2.at[0])))]
     act_loads = [pltpu.make_async_copy(s, d, ld_sem.at[3 + i]) for i, (s, d) in enumerate(((x_hbm, xv), (dy_hbm, dyv)))]
@@ -61,9 +62,9 @@
     g_load(1).start()
 
     barrier = pltpu.get_barrier_semaphore()
-    for d in (partner, x_nbr, y_nbr, *others):
+    for d in (partner, x_nbr, y_nbr, z_near, z_mirror):
         pl.semaphore_signal(barrier, inc=1, device_id=d, device_id_type=pl.DeviceIdType.MESH)
-    pl.semaphore_wait(barrier, 6)
+    pl.semaphore_wait(barrier, 5)
 
     def part(slot, p):
         if p < 2:
@@ -132,8 +133,8 @@
             src_ref=src, dst_ref=dst, send_sem=s_sem.at[stage, k % SLOTS], recv_sem=r_sem.at[stage, k],
             device_id=device, device_id_type=pl.DeviceIdType.MESH)
 
-    def quarter(zz):
-        return pl.ds(pl.multiple_of(zz % 4 * rq, rq), rq)
+    def half(other=0):
+        return pl.ds(pl.multiple_of((z + 1 + other) % 2 * rh, rh), rh)
 
     def stage_copy(stage, k):
         if stage == 0:
@@ -142,13 +143,14 @@
             return rcopy(1, k, own.at[k, pl.ds(2, 2)], recv_1.at[k], neighbour(k, 0))
         if stage == 2:
             return rcopy(2, k, own.at[k, 1], recv_2.at[k], neighbour(k, 1))
-        if stage < 6:
-            j = stage - 3
-            return rcopy(stage, k, own.at[k, 0, quarter(z + j + 1)], recv_z.at[k, j], others[j])
-        return rcopy(stage, k, res.at[k, quarter(z)], res.at[k, quarter(z)], others[stage - 6])
-
-    STARTS = ((0,), (1,), (2,), (3, 4, 5), (6, 7, 8))
-    NEEDS = ((), (0,), (1,), (2,), (3, 4, 5))
+        if stage == 3:
+            return rcopy(3, k, own.at[k, 0], recv_z1.at[k], z_near)
+        if stage == 4:
+            return rcopy(4, k, own.at[k, 0, half(1)], recv_z2.at[k], z_mirror)
+        if stage == 5:
+            return rcopy(5, k, res.at[k, half()], res.at[k, half()], z_mirror)
+        at = half(stage - 6)
+        return rcopy(stage, k, res.at[k, at], res.at[k, at], z_near)
 
     def free_slot(stage, k):
         @pl.when(k >= SLOTS)
@@ -158,12 +160,15 @@
     def add(p, q):
         return (p.astype(F32) + q.astype(F32)).astype(BF16)
 
+    def start(stage, k):
+        free_slot(stage, k)
+        stage_copy(stage, k).start()
+
     def event(stage, k):
-        for n in STARTS[stage]:
-            free_slot(n, k)
-        for n in NEEDS[stage]:
-            stage_copy(n, k).wait_recv()
+        if stage > 0:
+            stage_copy(stage - 1, k).wait_recv()
         if stage == 0:
+            free_slot(0, k)
             typ = k % 2
             g_load(k).wait()
 
@@ -178,25 +183,35 @@
                     block = yy * 4 + xx * 2
                     send_c[k % SLOTS, 2 * a + b] = gbuf[k % 3, :, pl.ds(pl.multiple_of((block + 1 - c) * wide, wide), wide)].astype(BF16)
                     own[k, 2 * a + b] = gbuf[k % 3, :, pl.ds(pl.multiple_of((block + c) * wide, wide), wide)].astype(BF16)
+            stage_copy(0, k).start()
         elif stage == 1:
             own[k] = add(own[k], recv_c[k])
+            start(1, k)
         elif stage == 2:
             own[k, 0:2] = add(own[k, 0:2], recv_1[k])
+            start(2, k)
         elif stage == 3:
             own[k, 0] = add(own[k, 0], recv_2[k])
+
+            @pl.when(inner == 0)
+            def _():
+                start(3, k)
+        elif stage == 4:
+            own[k, 0] = add(own[k, 0], recv_z1[k])
+            start(4, k)
+        elif stage == 5:
+            res[k, half()] = add(own[k, 0, half()], recv_z2[k])
+            start(5, k)
+            start(6, k)
         else:
-            total = own[k, 0, quarter(z)].astype(F32)
-            for j in range(3):
-                total += recv_z[k, j].astype(F32)
-            res[k, quarter(z)] = total.astype(BF16)
-        for n in STARTS[stage]:
-            stage_copy(n, k).start()
+            start(7, k)
 
     def reduce_events(u):
-        for stage in range(4, -1, -1):
+        for stage in range(6, -1, -1):
             k = u - FIRST - LAGS[stage]
-
-            @pl.when((k >= 0) & (k < CHUNKS))
+            here = (k >= 0) & (k < CHUNKS)
+
+            @pl.when(here if stage < 4 else here & (inner == 1))
             def _(stage=stage, k=k):
                 event(stage, k)
 
@@ -329,9 +344,12 @@
     after(UNITS - 1)
     lax.fori_loop(UNITS + 1, FIRST + CHUNKS + LAGS[-1], tail, 0)
 
-    for k in range(CHUNKS):
-        for n in (6, 7, 8):
-            stage_copy(n, k).wait_recv()
+    @pl.when(inner == 0)
+    def _():
+        for k in range(CHUNKS):
+            stage_copy(6, k).wait_recv()
+            stage_copy(7, k).wait_recv()
+
     store = pltpu.make_async_copy(res, dn_out, ld_sem.at[0])
     store.start()
 
@@ -349,9 +367,21 @@
     for p in range(4):
         for cp in take_x(p) + take_y(p) + take_d(p):
             cp.wait_send()
-    for stage in range(9):
-        for k in range(CHUNKS - SLOTS, CHUNKS):
-            stage_copy(stage, k).wait_send()
+    def drain(*stages):
+        for stage in stages:
+            for k in range(CHUNKS - SLOTS, CHUNKS):
+                stage_copy(stage, k).wait_send()
+
+    drain(0, 1, 2)
+
+    @pl.when(inner == 0)
+    def _():
+        drain(3)
+
+    @pl.when(inner == 1)
+    def _():
+        drain(4, 5, 6, 7)
+
     dw_copy(BLOCKS - 2).wait()
     dw_copy(BLOCKS - 1).wait()
     for m in range(TILES):
@@ -387,8 +417,8 @@
                 vm((3, rows, hidden), F32),
                 vm((SLOTS, 4, rows, wide), BF16), vm((CHUNKS, 4, rows, wide), BF16), vm((CHUNKS, 4, rows, wide), BF16),
                 vm((CHUNKS, 2, rows, wide), BF16), vm((CHUNKS, rows, wide), BF16),
-                vm((CHUNKS, 3, rows // 4, wide), BF16), vm((CHUNKS, rows, wide), BF16),
-                dma((5,)), dma((3,)), dma((10, 4)), dma((BLOCKS, 4)), dma((9, SLOTS)), dma((9, CHUNKS)), dma((2,)), dma((TILES,)),
+                vm((CHUNKS, rows, wide), BF16), vm((CHUNKS, rows // 2, wide), BF16), vm((CHUNKS, rows, wide), BF16),
+                dma((5,)), dma((3,)), dma((10, 4)), dma((BLOCKS, 4)), dma((8, SLOTS)), dma((8, CHUNKS)), dma((2,)), dma((TILES,)),
             ],
             compiler_params=pltpu.CompilerParams(collective_id=0, has_side_effects=True, vmem_limit_bytes=67043328),
             cost_estimate=pl.CostEstimate(flops=16 * tokens * dim * hidden, bytes_accessed=60 << 20, transcendentals=tokens * hidden),

time: 121 us -> 119 us (0.983)
  Pallas kernels: 103 us -> 101 us
    pallas_call x1, Pallas kernels: 103 us -> 101 us  [per_device(): pl.pallas_call(whole_step, out_shape=[jax.ShapeDtypeStruct((tokens, dim),...]
where the time goes in v5:
time: 119 us
  Pallas kernels  101 us (85%)
  local copies, waits for them, and re-layouts  14.7 us (12%)
  other arithmetic  3.03 us (3%)
    pallas_call x1, Pallas kernels, per_device(): pl.pallas_call(whole_step, out_shape=[jax.ShapeDtypeStruct((tokens, dim),...  101 us
    unnamed x4, local copies, waits for them, and re-layouts  14.7 us
    convert_element_type x1, other arithmetic, per_device(): return (dx, dn.reshape(3, dim, wide).astype(F32), dw[None])  3.03 us

profile of v5, /device:TPU:0, one launch (start us, length us, event | category | flops | bytes accessed | tf_op | source)
XLA Modules:
  0.0 118.9 jit_solution(7848662681289141010)
XLA Ops:
  0.6 100.6 %shard_map.85 = (bf16[2048,768]{1,0:T(8,128)(2,1)}, bf16[18,128,256]{2,1,0:T(8,128)(2,1)}, f32[3,768,2048]{2,1,0:T(8,128)}) custom-call(bf16[2048,768]{1,0:T(8,128)(2,1)} %x_hbm.1, bf16[2048,768]{1,0:T(8,128)(2,1)} %dy_hbm.1, bf16[768,256]{1,0:T(8,128)(2,1)} %wg_hbm.1, bf16[768,256]{1,0:T(8,128)(2,1)} %wu_hbm.1, bf16[256,768]{1,0:T(8,128)(2,1)} %wd_hbm.1, ...), custom_call_target="tpu_custom_call" | custom-call | flops 51539607552 | bytes 62914560 | tf_op jit(solution)/shard_map/pallas_call | solution.py:402
  101.2 0.0 copy-start
  101.2 3.0 %bitcast_convert_fusion = f32[3,768,256]{2,1,0:T(8,128)} fusion(bf16[3,768,256]{2,1,0:T(8,128)(2,1)} %bitcast.7), kind=kLoop, calls=%fused_computation | loop fusion | flops 589824 | bytes 3538944 | tf_op jit(solution)/shard_map/convert_element_type | solution.py:426
  104.2 0.0 copy-done
  104.2 1.7 %copy.11 = bf16[2048,768]{1,0:T(8,128)(2,1)} copy(bf16[2048,768]{1,0:T(8,128)(2,1)S(1)} %copy-done) | data formatting | bytes 6291456
  105.9 13.0 %copy.12 = f32[1,3,768,2048]{3,2,1,0:T(8,128)} copy(f32[1,3,768,2048]{3,2,1,0:T(8,128)} %bitcast.6) | data formatting | bytes 37748736
Async XLA Ops:
  101.2 3.0 %copy-start = (bf16[2048,768]{1,0:T(8,128)(2,1)S(1)}, bf16[2048,768]{1,0:T(8,128)(2,1)}, u32[]{:S(2)}) copy-start(bf16[2048,768]{1,0:T(8,128)(2,1)} %get-tuple-element.12) | copy-start | bytes 9437188

commit v6 on v5

--- a/solution.py
+++ b/solution.py
@@ -16,7 +16,10 @@
 BLOCKS = 8
 TILES = 4
 UNITS = BLOCKS * TILES
+KEPT = 5
+LATE = BLOCKS - KEPT
 CHUNKS = 18
+EXPORT = 10
 FIRST = 1
 LAGS = (0, 1, 4, 7, 11, 13, 15)
 TAKE_XY, TAKE_D = (2, 3, 4, 6), (10, 11, 14, 14)
@@ -26,10 +29,84 @@
 SLOTS = 4
 
 
-def whole_step(x_hbm, dy_hbm, wg_hbm, wu_hbm, wd_hbm, g_hbm, dx_out, dn_out, dw_out,
+def slot_at(i, act):
+    return jnp.where(i < 2, i, 2 + (i + 4 + 3 * (1 - act)) % 6)
+
+
+def column_at(slot, x, y, c):
+    b = jnp.where(slot < 5, slot, slot - 3)
+    dc = jnp.where((slot == 1) | (slot >= 5), 1, 0)
+    ddx = jnp.where((b == 2) | (b == 4), 1, 0)
+    ddy = jnp.where((b == 3) | (b == 4), 1, 0)
+    return ((y + ddy) % 2) * 4 + ((x + ddx) % 2) * 2 + (c + dc) % 2
+
+
+def finish(dx_in, dn_in, dw_in, dab_in, h_in, xt_in, dyt_in, dx_out, dn_out, dw_out,
+           dxv, dnb, dnf, slab, acc, dab, h, xt, dyt, in_sem, slab_sem, late_sem, out_sem):
+    z, y, f = lax.axis_index("dp"), lax.axis_index("row"), lax.axis_index("fsdp")
+    x, c = f // 2, f % 2
+    act = (z % 2 + c + 1) % 2
+    wide = slab.shape[3]
+
+    def columns(i):
+        return pl.ds(pl.multiple_of(column_at(slot_at(i, act), x, y, c) * wide, wide), wide)
+
+    def load_late(n):
+        at = pl.ds(n * TILES, TILES)
+        return [pltpu.make_async_copy(dab_in.at[at], dab.at[at], late_sem.at[0, n]), pltpu.make_async_copy(h_in.at[at], h.at[at], late_sem.at[1, n])]
+
+    def load_slab(i):
+        return pltpu.make_async_copy(dw_in.at[:, :, columns(i)], slab.at[i], slab_sem.at[i])
+
+    def store(i):
+        source = slab.at[i] if i < KEPT else acc.at[i - KEPT]
+        return pltpu.make_async_copy(source, dw_out.at[:, :, columns(i)], out_sem.at[i])
+
+    left = [pltpu.make_async_copy(xt_in, xt, in_sem.at[0]), pltpu.make_async_copy(dyt_in, dyt, in_sem.at[1])]
+    dx_load, dn_load = pltpu.make_async_copy(dx_in, dxv, in_sem.at[2]), pltpu.make_async_copy(dn_in, dnb, in_sem.at[3])
+    dx_store, dn_store = pltpu.make_async_copy(dxv, dx_out, out_sem.at[BLOCKS]), pltpu.make_async_copy(dnf, dn_out, out_sem.at[BLOCKS + 1])
+    for cp in left + load_late(0) + [load_slab(0), load_slab(1)] + load_late(1) + [load_slab(2)] + load_late(2) + [load_slab(3), load_slab(4), dx_load, dn_load]:
+        cp.start()
+    for cp in left:
+        cp.wait()
+    for n in range(LATE):
+        for cp in load_late(n):
+            cp.wait()
+
+        def tile_step(m, carry, n=n):
+            for a in range(2):
+                at = pl.ds(a * (xt.shape[1] // 2), xt.shape[1] // 2)
+                both = jnp.dot(xt[m, at], dab[n * TILES + m], preferred_element_type=F32)
+                third = jnp.dot(dyt[m, at], h[n * TILES + m], preferred_element_type=F32)
+                for t, part in enumerate((both[:, :wide], both[:, wide:], third)):
+                    acc[n, t, at] = jnp.where(m == 0, 0.0, acc[n, t, at]) + part
+            return carry
+
+        lax.fori_loop(0, TILES, tile_step, 0)
+        store(KEPT + n).start()
+        for i in range(2 * n, min(2 * n + 2, KEPT)):
+            load_slab(i).wait()
+            store(i).start()
+    dx_load.wait()
+    dx_store.start()
+    dn_load.wait()
+
+    def widen(k, carry):
+        dnf[k] = dnb[k].astype(F32)
+        return carry
+
+    lax.fori_loop(0, CHUNKS, widen, 0)
+    dn_store.start()
+    for i in range(BLOCKS):
+        store(i).wait()
+    dx_store.wait()
+    dn_store.wait()
+
+
+def whole_step(x_hbm, dy_hbm, wg_hbm, wu_hbm, wd_hbm, g_hbm, dx_out, dn_out, dw_out, dab_out, h_out, xt_out, dyt_out,
                xv, dyv, xt, dyt, w13, w2, dab_even, dab_odd, h_even, h_odd, dxacc, dwacc,
                gbuf, send_c, own, recv_c, recv_1, recv_2, recv_z1, recv_z2, res,
-               ld_sem, g_sem, ws_sem, wr_sem, s_sem, r_sem, dw_sem, out_sem):
+               ld_sem, g_sem, ws_sem, wr_sem, s_sem, r_sem, dw_sem, out_sem, keep_sem, ex_sem):
     z, y, f = lax.axis_index("dp"), lax.axis_index("row"), lax.axis_index("fsdp")
     x, c = f // 2, f % 2
     z0 = z % 2
@@ -230,14 +307,10 @@
                                     cp.start()
 
     def slot_of(i):
-        return jnp.where(i < 2, i, 2 + (i + 1 + 3 * (1 - act) + 3) % 6)
+        return slot_at(i, act)
 
     def column_of(slot):
-        b = jnp.where(slot < 5, slot, slot - 3)
-        dc = jnp.where((slot == 1) | (slot >= 5), 1, 0)
-        ddx = jnp.where((b == 2) | (b == 4), 1, 0)
-        ddy = jnp.where((b == 3) | (b == 4), 1, 0)
-        return ((y + ddy) % 2) * 4 + ((x + ddx) % 2) * 2 + (c + dc) % 2
+        return column_at(slot, x, y, c)
 
     def dw_copy(i):
         at = pl.ds(pl.multiple_of(column_of(slot_of(i)) * wide, wide), wide)
@@ -268,9 +341,14 @@
             xt[m] = xv[rows_of(m)].T
             dyt[m] = dyv[rows_of(m)].T
 
-        @pl.when((m == 1) & (i >= 2))
+        @pl.when((m == 1) & (i >= 2) & (i < KEPT + 2))
         def _():
             dw_copy(i - 2).wait()
+
+        @pl.when(u == EXPORT)
+        def _():
+            for cp in exports:
+                cp.start()
 
     def products(u):
         slot, at = slot_of(u // TILES), rows_of(u % TILES)
@@ -287,27 +365,36 @@
         dab[:, :wide] = (dh * b * s * (1.0 + a * (1.0 - s))).astype(BF16)
         dab[:, wide:] = (dh * silu).astype(BF16)
 
-    def gradients(u, dab, h):
+    exports = [pltpu.make_async_copy(xt, xt_out, ex_sem.at[0]), pltpu.make_async_copy(dyt, dyt_out, ex_sem.at[1])]
+
+    def keep(u, parity):
+        dab, h = (even, odd)[parity]
+        n = u - KEPT * TILES
+        return [pltpu.make_async_copy(dab, dab_out.at[n], keep_sem.at[0, parity]), pltpu.make_async_copy(h, h_out.at[n], keep_sem.at[1, parity])]
+
+    def gradients(u, dab, h, late=False):
         i, m = u // TILES, u % TILES
         d = i % 2
         half, dim = tile // 2, xt.shape[1] // 2
         first = pl.multiple_of(m * tile, tile)
-        for n in range(2):
-            at = pl.ds(n * dim, dim)
-            dwacc[d, 2, at] = jnp.where(m == 0, 0.0, dwacc[d, 2, at]) + dot(dyt[m, at], h[...], FIRST_TO_LAST)
+        if not late:
+            for n in range(2):
+                at = pl.ds(n * dim, dim)
+                dwacc[d, 2, at] = jnp.where(m == 0, 0.0, dwacc[d, 2, at]) + dot(dyt[m, at], h[...], FIRST_TO_LAST)
         for n in range(2):
             at = pl.ds(first + n * half, half)
             dxacc[at] = jnp.where(i == 0, 0.0, dxacc[at]) + dot(dab[n * half:(n + 1) * half], w13[slot_of(i)], LAST)
-        for n in range(2):
-            at = pl.ds(n * dim, dim)
-            left = dot(xt[m, at], dab[...], FIRST_TO_LAST)
-            dwacc[d, 0, at] = jnp.where(m == 0, 0.0, dwacc[d, 0, at]) + left[:, :wide]
-            dwacc[d, 1, at] = jnp.where(m == 0, 0.0, dwacc[d, 1, at]) + left[:, wide:]
+        if not late:
+            for n in range(2):
+                at = pl.ds(n * dim, dim)
+                left = dot(xt[m, at], dab[...], FIRST_TO_LAST)
+                dwacc[d, 0, at] = jnp.where(m == 0, 0.0, dwacc[d, 0, at]) + left[:, :wide]
+                dwacc[d, 1, at] = jnp.where(m == 0, 0.0, dwacc[d, 1, at]) + left[:, wide:]
 
     def after(u):
         i, m = u // TILES, u % TILES
 
-        @pl.when(m == TILES - 1)
+        @pl.when((m == TILES - 1) & (i < KEPT))
         def _():
             dw_copy(i).start()
 
@@ -319,16 +406,29 @@
 
     even, odd = (dab_even, h_even), (dab_odd, h_odd)
 
-    def step(u, now, last):
+    def step(u, parity, late=False):
+        now, last = (even, odd)[parity], (even, odd)[1 - parity]
         before(u)
+        if late:
+            @pl.when(u >= KEPT * TILES + 2)
+            def _():
+                for cp in keep(u - 2, parity):
+                    cp.wait()
+            for cp in keep(u - 1, 1 - parity):
+                cp.start()
         ab, dh = products(u)
-        gradients(u - 1, *last)
+        gradients(u - 1, *last, late)
         gate(ab, dh, *now)
         after(u - 1)
 
     def body(v, carry):
-        step(2 * v + 1, odd, even)
-        step(2 * v + 2, even, odd)
+        step(2 * v + 1, 1)
+        step(2 * v + 2, 0)
+        return carry
+
+    def late_body(v, carry):
+        step(2 * v + 1, 1, True)
+        step(2 * v + 2, 0, True)
         return carry
 
     def tail(u, carry):
@@ -337,10 +437,13 @@
 
     before(0)
     gate(*products(0), *even)
-    lax.fori_loop(0, UNITS // 2 - 1, body, 0)
-    step(UNITS - 1, odd, even)
+    lax.fori_loop(0, KEPT * TILES // 2, body, 0)
+    lax.fori_loop(KEPT * TILES // 2, UNITS // 2 - 1, late_body, 0)
+    step(UNITS - 1, 1, True)
+    for cp in keep(UNITS - 1, 1):
+        cp.start()
     reduce_events(UNITS)
-    gradients(UNITS - 1, *odd)
+    gradients(UNITS - 1, *odd, True)
     after(UNITS - 1)
     lax.fori_loop(UNITS + 1, FIRST + CHUNKS + LAGS[-1], tail, 0)
 
@@ -382,8 +485,8 @@
     def _():
         drain(4, 5, 6, 7)
 
-    dw_copy(BLOCKS - 2).wait()
-    dw_copy(BLOCKS - 1).wait()
+    for cp in keep(UNITS - 2, 0) + keep(UNITS - 1, 1) + exports:
+        cp.wait()
     for m in range(TILES):
         dx_copy(m).wait()
     store.wait()
@@ -399,15 +502,19 @@
         g = g_part.reshape(CHUNKS, rows, hidden)
         vm = pltpu.VMEM
         dma = pltpu.SemaphoreType.DMA
-        dx, dn, dw = pl.pallas_call(
+        made = pl.pallas_call(
             whole_step,
             out_shape=[
                 jax.ShapeDtypeStruct((tokens, dim), BF16),
                 jax.ShapeDtypeStruct((CHUNKS, rows, wide), BF16),
                 jax.ShapeDtypeStruct((3, dim, hidden), F32),
+                jax.ShapeDtypeStruct((LATE * TILES, tile, 2 * wide), BF16),
+                jax.ShapeDtypeStruct((LATE * TILES, tile, wide), BF16),
+                jax.ShapeDtypeStruct((TILES, dim, tile), BF16),
+                jax.ShapeDtypeStruct((TILES, dim, tile), BF16),
             ],
             in_specs=[pl.BlockSpec(memory_space=pl.ANY)] * 6,
-            out_specs=[pl.BlockSpec(memory_space=pl.ANY)] * 3,
+            out_specs=[pl.BlockSpec(memory_space=pl.ANY)] * 7,
             scratch_shapes=[
                 vm((tokens, dim), BF16), vm((tokens, dim), BF16),
                 vm((TILES, dim, tile), BF16), vm((TILES, dim, tile), BF16),
@@ -418,12 +525,31 @@
                 vm((SLOTS, 4, rows, wide), BF16), vm((CHUNKS, 4, rows, wide), BF16), vm((CHUNKS, 4, rows, wide), BF16),
                 vm((CHUNKS, 2, rows, wide), BF16), vm((CHUNKS, rows, wide), BF16),
                 vm((CHUNKS, rows, wide), BF16), vm((CHUNKS, rows // 2, wide), BF16), vm((CHUNKS, rows, wide), BF16),
-                dma((5,)), dma((3,)), dma((10, 4)), dma((BLOCKS, 4)), dma((8, SLOTS)), dma((8, CHUNKS)), dma((2,)), dma((TILES,)),
+                dma((5,)), dma((3,)), dma((10, 4)), dma((BLOCKS, 4)), dma((8, SLOTS)), dma((8, CHUNKS)), dma((2,)), dma((TILES,)), dma((2, 2)), dma((2,)),
             ],
             compiler_params=pltpu.CompilerParams(collective_id=0, has_side_effects=True, vmem_limit_bytes=67043328),
             cost_estimate=pl.CostEstimate(flops=16 * tokens * dim * hidden, bytes_accessed=60 << 20, transcendentals=tokens * hidden),
         )(x_blk, dy_blk, gate, up, down, g)
-        return dx, dn.reshape(3, dim, wide).astype(F32), dw[None]
+        dx, dn, dw = pl.pallas_call(
+            finish,
+            out_shape=[
+                jax.ShapeDtypeStruct((tokens, dim), BF16),
+                jax.ShapeDtypeStruct((CHUNKS, rows, wide), F32),
+                jax.ShapeDtypeStruct((3, dim, hidden), F32),
+            ],
+            in_specs=[pl.BlockSpec(memory_space=pl.ANY)] * 7,
+            out_specs=[pl.BlockSpec(memory_space=pl.ANY)] * 3,
+            scratch_shapes=[
+                vm((tokens, dim), BF16), vm((CHUNKS, rows, wide), BF16), vm((CHUNKS, rows, wide), F32),
+                vm((KEPT, 3, dim, wide), F32), vm((LATE, 3, dim, wide), F32),
+                vm((LATE * TILES, tile, 2 * wide), BF16), vm((LATE * TILES, tile, wide), BF16),
+                vm((TILES, dim, tile), BF16), vm((TILES, dim, tile), BF16),
+                dma((4,)), dma((KEPT,)), dma((2, LATE)), dma((BLOCKS + 2,)),
+            ],
+            compiler_params=pltpu.CompilerParams(vmem_limit_bytes=67043328),
+            cost_estimate=pl.CostEstimate(flops=2 * tokens * dim * hidden, bytes_accessed=56 << 20, transcendentals=0),
+        )(*made)
+        return dx, dn.reshape(3, dim, wide), dw[None]
 
     return jax.shard_map(
         per_device,

time: 119 us -> 118 us (level)
  Pallas kernels: 101 us -> 117 us
  local copies, waits for them, and re-layouts: 14.7 us -> 0 us
  other arithmetic: 3.03 us -> 0 us
    pallas_call x0 -> x1, Pallas kernels: none -> 19.3 us  [per_device(): pl.pallas_call(finish, out_shape=[jax.ShapeDtypeStruct((tokens, dim), BF1...]
    unnamed x4 -> x0, local copies, waits for them, and re-layouts: 14.7 us -> none
    pallas_call x1, Pallas kernels: 101 us -> 97.4 us  [per_device(): pl.pallas_call(whole_step, out_shape=[jax.ShapeDtypeStruct((tokens, dim),...]
    convert_element_type x1 -> x0, other arithmetic: 3.03 us -> none  [per_device(): return (dx, dn.reshape(3, dim, wide).astype(F32), dw[None])]
where the time goes in v6:
time: 118 us
  Pallas kernels  117 us (99%)
    pallas_call x1, Pallas kernels, per_device(): pl.pallas_call(whole_step, out_shape=[jax.ShapeDtypeStruct((tokens, dim),...  97.4 us
    pallas_call x1, Pallas kernels, per_device(): pl.pallas_call(finish, out_shape=[jax.ShapeDtypeStruct((tokens, dim), BF1...  19.3 us

profile of v6, /device:TPU:0, one launch (start us, length us, event | category | flops | bytes accessed | tf_op | source)
XLA Modules:
  0.0 117.5 jit_solution(7476707448491054137)
XLA Ops:
  0.6 97.4 %shard_map.85 = (bf16[2048,768]{1,0:T(8,128)(2,1)}, bf16[18,128,256]{2,1,0:T(8,128)(2,1)}, f32[3,768,2048]{2,1,0:T(8,128)}, bf16[12,512,512]{2,1,0:T(8,128)(2,1)...) custom-call(bf16[2048,768]{1,0:T(8,128)(2,1)} %x_hbm.1, ...), custom_call_target="tpu_custom_call" | custom-call | flops 51539607552 | bytes 62914560 | tf_op jit(solution)/shard_map/pallas_call | solution.py:505
  98.1 19.3 %shard_map.86 = (bf16[2048,768]{1,0:T(8,128)(2,1)}, f32[18,128,256]{2,1,0:T(8,128)}, f32[3,768,2048]{2,1,0:T(8,128)}) custom-call(bf16[2048,768]{1,0:T(8,128)(2,1)} %get-tuple-element.13.dx_in, bf16[18,128,256]{2,1,0:T(8,128)(2,1)} %get-tuple-element.14.dn_in, f32[3,768,2048]{2,1,0:T(8,128)} %get-tuple-element.15.dw_in, ...), custom_call_target="tpu_custom_call" | custom-call | flops 6442450944 | bytes 58720256 | tf_op jit(solution)/shard_map/pallas_call | solution.py:533

commit v7 on v6

--- a/solution.py
+++ b/solution.py
@@ -21,10 +21,10 @@
 CHUNKS = 18
 EXPORT = 10
 FIRST = 1
-LAGS = (0, 1, 4, 7, 11, 13, 15)
-TAKE_XY, TAKE_D = (2, 3, 4, 6), (10, 11, 14, 14)
-Z_X, Z_Y = (2, 3, 4, 6), (4, 6, 10, 15)
-PASS_X, PASS_Y, PASS_D = (10, 10, 13, 13), (14, 14, 16, 17), (22, 25, 27, 27)
+LAGS = (0, 1, 5, 9, 12, 14, 16)
+TAKE_XY, TAKE_D = (2, 3, 5, 7), (9, 12, 12, 13)
+Z_X, Z_Y = (2, 3, 5, 9), (3, 3, 7, 12)
+PASS_X, PASS_Y, PASS_D = (8, 8, 12, 12), (13, 13, 15, 16), (20, 23, 26, 26)
 GROUP = 4
 SLOTS = 4
 

time: 118 us -> 116 us (0.983)
  Pallas kernels: 117 us -> 115 us
    pallas_call x1, Pallas kernels: 97.4 us -> 95.5 us  [per_device(): pl.pallas_call(whole_step, out_shape=[jax.ShapeDtypeStruct((tokens, dim),...]
where the time goes in v7:
time: 116 us
  Pallas kernels  115 us (99%)
    pallas_call x1, Pallas kernels, per_device(): pl.pallas_call(whole_step, out_shape=[jax.ShapeDtypeStruct((tokens, dim),...  95.5 us
    pallas_call x1, Pallas kernels, per_device(): pl.pallas_call(finish, out_shape=[jax.ShapeDtypeStruct((tokens, dim), BF1...  19.3 us

profile of v7, /device:TPU:0, one launch (start us, length us, event | category | flops | bytes accessed | tf_op | source)
XLA Modules:
  0.0 115.6 jit_solution(10405581926543332745)
XLA Ops:
  0.6 95.5 %shard_map.85 = (bf16[2048,768]{1,0:T(8,128)(2,1)}, bf16[18,128,256]{2,1,0:T(8,128)(2,1)}, f32[3,768,2048]{2,1,0:T(8,128)}, bf16[12,512,512]{2,1,0:T(8,128)(2,1)...) custom-call(bf16[2048,768]{1,0:T(8,128)(2,1)} %x_hbm.1, ...), custom_call_target="tpu_custom_call" | custom-call | flops 51539607552 | bytes 62914560 | tf_op jit(solution)/shard_map/pallas_call | solution.py:505
  96.1 19.3 %shard_map.86 = (bf16[2048,768]{1,0:T(8,128)(2,1)}, f32[18,128,256]{2,1,0:T(8,128)}, f32[3,768,2048]{2,1,0:T(8,128)}) custom-call(bf16[2048,768]{1,0:T(8,128)(2,1)} %get-tuple-element.13.dx_in, bf16[18,128,256]{2,1,0:T(8,128)(2,1)} %get-tuple-element.14.dn_in, f32[3,768,2048]{2,1,0:T(8,128)} %get-tuple-element.15.dw_in, ...), custom_call_target="tpu_custom_call" | custom-call | flops 6442450944 | bytes 58720256 | tf_op jit(solution)/shard_map/pallas_call | solution.py:533
